TPU v7x, 32 devices: a whole 2x2x4 slice. The times are simulated.
32 devices in a mesh: dom: 8 (over y, x, core), rep: 4 (over z).
Axes of the slice: x: 2, y: 2, z: 4, core: 2. Of those that a mesh axis runs over, the one named last changes fastest.
Arguments:
- hop_feats: bfloat16 [3, 65536, 128], P(None, ('dom', 'rep')), may hold values from -6 to 6
- adj_local: bfloat16 [512, 12, 128, 128], P(('dom', 'rep')), may hold values from -0.125 to 0.125
- local_cols: int32 [512, 12], P(('dom', 'rep')), may hold values from 0 to 15
- adj_halo: bfloat16 [512, 4, 128, 128], P(('dom', 'rep')), may hold values from -0.125 to 0.125
- halo_cols: int32 [512, 4], P(('dom', 'rep')), may hold values from 0 to 3
- boundary_rows: int32 [32, 512], P(('dom', 'rep')), may hold values from 0 to 2047
- train_ids: int32 [32, 2048], P(('dom', 'rep')), may hold values from 0 to 2047, as said below
- shuffle: int32 [32, 2048], P(('dom', 'rep')), may hold values from 0 to 2047, as said below
- labels: int32 [65536], P(('dom', 'rep')), may hold values from 0 to 171
- labelled: int32 [65536], P(('dom', 'rep')), may hold values from 0 to 1
- w_first: bfloat16 [512, 1024], P(None, 'rep'), may hold values from -1 to 1
- w_second: bfloat16 [1024, 172], P('rep'), may hold values from -2 to 2
Outputs:
- next_hop: bfloat16 [65536, 128], P(('dom', 'rep'))
- batch_loss: float32 [32, 32], P(('dom', 'rep'))
- grad_first: float32 [512, 1024], P('dom', 'rep')
- grad_second: float32 [1024, 172], P('rep')
Inputs may be any that keep to these rules, and one draw needn't show every extreme that they name: `local_cols`: local tile indices of the partition's own row tiles. `halo_cols`: indices of received boundary tiles. `boundary_rows`: rows of the sending partition itself. `train_ids`: rows of the partition itself. `shuffle`: each row is a permutation of 0 .. 2047.
All inputs are finite; a program needn't handle non-finite values.
Results may differ from a plain program's by a relative error of at most 0.005.
The roundings to bfloat16 on the way count: a program that leaves them out, or rounds other values in their place, can miss the bound.
Values may be sent and summed in bfloat16 or wider, within the bound.
A program may use at most 128 MiB of HBM per device.

v0:
```python
import jax
import jax.numpy as jnp
from jax import lax
from jax.sharding import PartitionSpec as P


def loss_head(logits, targets, weights_row):
    row_max = jnp.max(logits, axis=1, keepdims=True)
    expos = jnp.exp(logits - row_max)
    totals = jnp.sum(expos, axis=1, keepdims=True)
    classes = lax.broadcasted_iota(jnp.int32, logits.shape, 1)
    onehot = (classes == targets[:, None]).astype(jnp.float32)
    cross = jnp.log(totals[:, 0]) + row_max[:, 0] - jnp.sum(onehot * logits, axis=1)
    count = jnp.maximum(jnp.sum(weights_row), 1.0)
    dlogits = ((expos / totals - onehot) * (weights_row / count)[:, None]).astype(jnp.bfloat16)
    return (cross, dlogits)


def source_losses(cross, weights_row, groups):
    masks = weights_row.reshape(groups, -1)
    sums = jnp.sum(masks * cross.reshape(groups, -1), axis=1)
    return sums / jnp.maximum(jnp.sum(masks, axis=1), 1.0)


def batch_norm(pre):
    center = pre - jnp.mean(pre, axis=-2, keepdims=True)
    rstd = lax.rsqrt(jnp.mean(center * center, axis=-2, keepdims=True) + 1e-05)
    return (center * rstd, rstd)


def norm_back(grad, normed, rstd):
    mean_grad = jnp.mean(grad, axis=-2, keepdims=True)
    mean_proj = jnp.mean(grad * normed, axis=-2, keepdims=True)
    return (grad - mean_grad - normed * mean_proj) * rstd


def contract_rows(left, right):
    return lax.dot_general(
        left, right, (((0,), (0,)), ((), ())), preferred_element_type=jnp.float32
    )


def shards(
    hop_feats,
    adj_local,
    local_cols,
    adj_halo,
    halo_cols,
    boundary_rows,
    train_ids,
    shuffle,
    labels,
    labelled,
    w_first,
    w_second,
):
    num_dom = lax.axis_size("dom")
    num_rep = lax.axis_size("rep")
    devices = num_dom * num_rep
    tile = adj_local.shape[-1]
    row_tiles = adj_local.shape[0]
    rows = row_tiles * tile
    width = hop_feats.shape[2]
    hop_two = hop_feats[2]
    sent = jnp.take(hop_two, boundary_rows[0], axis=0)
    halo = lax.all_to_all(sent, ("dom", "rep"), split_axis=0, concat_axis=0, tiled=True)
    halo_count = halo.shape[0] // tile
    own_tiles = hop_two.reshape(row_tiles, tile, width)
    near = jnp.take(own_tiles, local_cols, axis=0)
    summed = jnp.einsum("ikab,ikbc->iac", adj_local, near, preferred_element_type=jnp.float32)
    far = jnp.take(halo.reshape(halo_count, tile, width), halo_cols, axis=0)
    summed = summed + jnp.einsum(
        "ikab,ikbc->iac", adj_halo, far, preferred_element_type=jnp.float32
    )
    next_hop = summed.reshape(rows, width).astype(jnp.bfloat16)
    order = jnp.take(train_ids[0], shuffle[0], axis=0)
    allfeat = jnp.concatenate([hop_feats[0], hop_feats[1], hop_two, next_hop], axis=1)
    feats = jnp.take(allfeat, order, axis=0)
    own_labels = jnp.take(labels, order, axis=0)
    own_marks = jnp.take(labelled, order, axis=0)
    target_pair = jnp.stack([own_labels, own_marks], axis=0)
    batch = lax.all_to_all(feats, ("dom", "rep"), split_axis=0, concat_axis=0, tiled=True)
    got_pair = lax.all_to_all(target_pair, ("dom", "rep"), split_axis=1, concat_axis=1, tiled=True)
    targets = got_pair[0]
    weights_row = got_pair[1].astype(jnp.float32)
    first_whole, second_whole = (
        lax.all_gather(w_first, "rep", axis=1, tiled=True),
        lax.all_gather(w_second, "rep", axis=0, tiled=True),
    )
    hidden_pre = jnp.dot(batch, first_whole, preferred_element_type=jnp.float32)
    normed, rstd = batch_norm(hidden_pre)
    hidden = jnp.maximum(normed, 0.0).astype(jnp.bfloat16)
    logits = jnp.dot(hidden, second_whole, preferred_element_type=jnp.float32)
    cross, dlogits = loss_head(logits, targets, weights_row)
    grad_two_full = contract_rows(hidden, dlogits)
    dhidden = lax.dot_general(
        dlogits, second_whole, (((1,), (1,)), ((), ())), preferred_element_type=jnp.float32
    )
    masked = jnp.where(normed > 0, dhidden, 0.0)
    dpre = norm_back(masked, normed, rstd).astype(jnp.bfloat16)
    grad_one_full = contract_rows(batch, dpre)
    grad_one_rep, grad_two_rep = (
        lax.psum_scatter(grad_one_full, "rep", scatter_dimension=1, tiled=True),
        lax.psum_scatter(grad_two_full, "rep", scatter_dimension=0, tiled=True),
    )
    grad_one = lax.psum_scatter(grad_one_rep, "dom", scatter_dimension=0, tiled=True)
    grad_two = lax.psum(grad_two_rep, "dom")
    loss = source_losses(cross, weights_row, devices)
    return (next_hop, loss.reshape(1, devices), grad_one, grad_two)


def solution(mesh):
    placed = (
        P(None, ("dom", "rep"), None),
        P(("dom", "rep"), None, None, None),
        P(("dom", "rep"), None),
        P(("dom", "rep"), None, None, None),
        P(("dom", "rep"), None),
        P(("dom", "rep"), None),
        P(("dom", "rep"), None),
        P(("dom", "rep"), None),
        P(("dom", "rep")),
        P(("dom", "rep")),
        P(None, "rep"),
        P("rep", None),
    )
    return jax.shard_map(
        shards,
        mesh=mesh,
        in_specs=placed,
        out_specs=(
            P(("dom", "rep"), None),
            P(("dom", "rep"), None),
            P("dom", "rep"),
            P("rep", None),
        ),
        check_vma=False,
    )
```

profile of v0, /device:TPU:0, one launch (start us, length us, event | category | flops | bytes accessed | tf_op | source)
XLA Modules:
  0.0 375.0 jit_solution(16362593156664925678)
XLA Ops:
  7.2 0.8 compare_select_fusion.5
  8.0 0.5 broadcast.147
  8.5 1.3 reduce.13
  10.0 2.6 slice_bitcast_fusion.1
  12.7 1.3 gather_fusion.1
  14.0 0.8 broadcast_select_fusion.1
  14.8 7.3 %all-to-all-start = ((bf16[32,16,128]{2,1,0:T(8,128)(2,1)}), bf16[32,16,128]{2,1,0:T(8,128)(2,1)S(1)}, u32[]{:S(2)}, u32[]{:S(2)}) async-start(bf16[32,16,128]{2,1,0:T(8,128)(2,1)} %broadcast_select_fusion.1), calls=%async_computation | async-start | bytes 262144 | tf_op jit(solution)/shard_map/all_to_all | solution.py:66
  22.4 11.8 %gather_fusion.4 = s32[2048]{0:T(1024)S(1)} fusion(s32[2048]{0:T(1024)S(1)} %bitcast.44, s32[2048]{0:T(1024)S(1)} %fusion.25), kind=kCustom, calls=%fused_computation.clone | custom fusion | bytes 24576 | tf_op jit(solution)/shard_map/jit(_take)/gather | solution.py:76
  34.2 0.7 copy-done.2
  34.9 11.8 %gather_fusion.6 = s32[2048]{0:T(1024)S(1)} fusion(s32[2048]{0:T(1024)S(1)} %copy-done.2, s32[2048]{0:T(1024)S(1)} %broadcast_clamp_fusion), kind=kCustom, calls=%fused_computation.2.clone | custom fusion | bytes 24576 | tf_op jit(solution)/shard_map/jit(_take)/gather | solution.py:80
  46.7 11.8 %gather_fusion.5 = s32[2048]{0:T(1024)S(1)} fusion(s32[2048]{0:T(1024)S(1)} %copy-done.3, s32[2048]{0:T(1024)S(1)} %broadcast_clamp_fusion), kind=kCustom, calls=%fused_computation.1.clone | custom fusion | bytes 24576 | tf_op jit(solution)/shard_map/jit(_take)/gather | solution.py:79
  59.0 0.7 reshape.253
  59.7 8.0 %gather_fusion = bf16[192,128,128]{2,1,0:T(8,128)(2,1)} fusion(bf16[16,128,128]{2,1,0:T(8,128)(2,1)S(1)} %bitcast.45, s32[1024]{0:T(1024)S(1)} %pad_clamp_fusion.2), kind=kCustom, calls=%fused_computation.3 | custom fusion | bytes 12583680 | tf_op jit(solution)/shard_map/jit(_take)/gather | solution.py:69
  67.7 5.8 %all-to-all-start.1 = ((s32[32,1,128]{2,1,0:T(1,128)}), s32[32,1,128]{2,1,0:T(1,128)S(1)}, u32[]{:S(2)}, u32[]{:S(2)}) async-start(s32[32,1,128]{2,1,0:T(1,128)} %reshape.253), calls=%async_computation.1 | async-start | bytes 32768 | tf_op jit(solution)/shard_map/all_to_all | solution.py:83
  73.6 2.2 gather_fusion.2
  75.7 2.4 fusion.9
  78.1 6.6 %fusion.18 = bf16[16,128,128]{1,2,0:T(8,128)(2,1)S(1)} fusion(f32[16,128,128]{1,2,0:T(8,128)S(1)} %fusion.9, bf16[16,12,128,128]{3,2,1,0:T(8,128)(2,1)} %param.15, bf16[16,12,128,128]{3,2,1,0:T(8,128)(2,1)} %bitcast.48, pred[16,12]{1,0:T(8,128)(4,1)S(1)} %compare_and_fusion.2), kind=kOutput, calls=%fused_computation.31 | convolution fusion | flops 808976384 | bytes 14155968 | tf_op jit(solution)/shard_map/ikab,ikbc->iac/dot_general | solution.py:70
  84.7 0.8 copy-done.8
  85.5 1.6 pad_maximum_fusion
  87.1 11.1 %gather_fusion.3 = bf16[2048,512]{1,0:T(8,128)(2,1)} fusion(bf16[2048,512]{1,0:T(8,128)(2,1)} %pad_maximum_fusion, s32[2048]{0:T(1024)S(1)} %broadcast_clamp_fusion), kind=kCustom, calls=%fused_computation.6 | custom fusion | bytes 4202496 | tf_op jit(solution)/shard_map/jit(_take)/gather | solution.py:78
  98.2 2.8 broadcast_select_fusion
  101.0 6.0 %all-to-all-start.2 = ((bf16[32,64,512]{2,1,0:T(8,128)(2,1)}), bf16[32,64,512]{2,1,0:T(8,128)(2,1)}, u32[]{:S(2)}, u32[]{:S(2)}) async-start(bf16[32,64,512]{2,1,0:T(8,128)(2,1)} %broadcast_select_fusion), calls=%async_computation.2 | async-start | bytes 4194304 | tf_op jit(solution)/shard_map/all_to_all | solution.py:82
  107.0 0.7 all-gather.2.cloned.1.call-update
  107.7 73.9 %all_gather.7 = bf16[1024,172]{0,1:T(8,128)(2,1)} all-gather(bf16[256,172]{0,1:T(8,128)(2,1)S(1)} %copy-done.9), channel_id=1, replica_groups=mesh['dom'=8,'rep'=4] {'rep'}, dimensions={0}, use_global_device_ids=true | all-gather | bytes 440320 | tf_op jit(solution)/shard_map/all_gather | solution.py:88
  181.7 0.5 broadcast.150
  182.2 0.7 reduce.14
  183.0 0.6 fusion.32
  184.3 0.8 divide_reduce_fusion
  185.1 0.7 div.54
  185.8 0.6 slice_reduce_fusion
  186.4 0.7 eq.10
  187.1 4.2 %fusion.35 = (f32[1024]{0:T(1024)S(1)}, f32[2048,1024]{1,0:T(8,128)S(1)}) fusion(bf16[2048,512]{1,0:T(8,128)(2,1)} %bitcast.21, bf16[512,1024]{1,0:T(8,128)(2,1)} %all-gather.2.cloned.1.call-done), kind=kOutput, calls=%fused_computation.77 | convolution fusion | flops 2149579776 | bytes 11538432 | tf_op jit(solution)/shard_map/dot_general | solution.py:90
  191.3 0.9 multiply_reduce_fusion.1
  192.2 0.3 copy-done.7
  192.6 1.6 fusion.36
  194.2 1.0 fusion.21
  195.2 0.6 copy-done.13
  195.8 2.5 fusion.23
  198.3 7.4 %fusion = (f32[1024]{0:T(1024)}, f32[1024]{0:T(1024)}, f32[2048,1024]{1,0:T(8,128)}) fusion(f32[2048,1024]{1,0:T(8,128)} %copy-done.4, f32[1024]{0:T(1024)S(1)} %add_rsqrt_fusion, f32[1024]{0:T(1024)S(1)} %broadcast_multiply_fusion.2, bf16[1024,172]{0,1:T(8,128)(2,1)} %all_gather.7, f32[2048,172]{0,1:T(8,128)S(1)} %get-tuple-element.22, f32[2048]{0:T(1024)} %div.54, ...), kind=kOutput, calls=%fused_computation.13 | convolution fusion | flops 738564096 | bytes 18587648 | tf_op jit(solution)/shard_map/dot_general | solution.py:96
  205.8 0.7 broadcast_multiply_fusion
  206.4 10.6 %fusion.4 = f32[512,1024]{1,0:T(8,128)} fusion(bf16[2048,512]{1,0:T(8,128)(2,1)} %bitcast.21, f32[2048,1024]{1,0:T(8,128)} %get-tuple-element.23, f32[2048,1024]{1,0:T(8,128)} %copy-done.4, f32[1024]{0:T(1024)S(1)} %get-tuple-element.24, f32[1024]{0:T(1024)S(1)} %get-tuple-element.25, f32[1024]{0:T(1024)S(1)} %add_rsqrt_fusion, ...), kind=kOutput, calls=%fused_computation.17 | convolution fusion | flops 2166358016 | bytes 20987904 | tf_op jit(solution)/shard_map/dot_general | solution.py:38
  217.2 11.8 %reduce-scatter.8.cloned.1.call-done = f32[256,172]{0,1:T(8,128)} async-done(((f32[1024,172]{0,1:T(8,128)}), f32[256,172]{0,1:T(8,128)}) %reduce-scatter.8.cloned.1.call-update) | async-done | bytes 176144 | tf_op jit(solution)/shard_map/reduce_scatter | solution.py:104
  229.0 44.9 %reduce-scatter.4.cloned.1.call-done = f32[512,256]{1,0:T(8,128)} async-done(((f32[512,1024]{1,0:T(8,128)}), f32[512,256]{1,0:T(8,128)}) %reduce-scatter.4.cloned.1.call-update) | async-done | bytes 524304 | tf_op jit(solution)/shard_map/reduce_scatter | solution.py:103
  274.1 0.1 multiply_reduce_fusion.2
  274.2 0.5 fusion.26
  274.7 54.4 %all-reduce.2.cloned.1.call-done = f32[256,172]{0,1:T(8,128)} async-done(((f32[256,172]{0,1:T(8,128)}), f32[256,172]{0,1:T(8,128)}) %all-reduce.2.cloned.1.call-update) | async-done | bytes 176144 | tf_op jit(solution)/shard_map/psum | solution.py:107
  329.1 37.7 %reduce-scatter.6.cloned.1.call-done = f32[64,256]{1,0:T(8,128)} async-done(((f32[512,256]{1,0:T(8,128)}), f32[64,256]{1,0:T(8,128)}) %reduce-scatter.6.cloned.1.call-update) | async-done | bytes 65552 | tf_op jit(solution)/shard_map/reduce_scatter | solution.py:106
  366.9 1.6 copy.25
  (75 shorter events, 1.3 us)
Async XLA Ops:
  7.2 68.6 %copy-start = (bf16[16,4,128,128]{3,2,1,0:T(8,128)(2,1)S(1)}, bf16[16,4,128,128]{3,2,1,0:T(8,128)(2,1)}, u32[]{:S(2)}) copy-start(bf16[16,4,128,128]{3,2,1,0:T(8,128)(2,1)} %param.17) | copy-start | bytes 6291460
  10.0 12.1 %copy-start.18 = (s32[16,4]{0,1:T(4,128)S(1)}, s32[16,4]{0,1:T(4,128)}, u32[]{:S(2)}) copy-start(s32[16,4]{0,1:T(4,128)} %param.18) | copy-start | bytes 772
  10.0 12.4 %copy-start.10 = (s32[1,2048]{1,0:T(1,128)S(1)}, s32[1,2048]{1,0:T(1,128)}, u32[]{:S(2)}) copy-start(s32[1,2048]{1,0:T(1,128)} %param.21) | copy-start | bytes 24580
  10.0 12.4 %copy-start.1 = (s32[1,2048]{1,0:T(1,128)S(1)}, s32[1,2048]{1,0:T(1,128)}, u32[]{:S(2)}) copy-start(s32[1,2048]{1,0:T(1,128)} %param.20) | copy-start | bytes 24580
  14.8 52.9 %all-to-all-start = ((bf16[32,16,128]{2,1,0:T(8,128)(2,1)}), bf16[32,16,128]{2,1,0:T(8,128)(2,1)S(1)}, u32[]{:S(2)}, u32[]{:S(2)}) async-start(bf16[32,16,128]{2,1,0:T(8,128)(2,1)} %broadcast_select_fusion.1), calls=%async_computation | async-start | bytes 262144 | tf_op jit(solution)/shard_map/all_to_all | solution.py:66
  34.2 0.7 copy-start.2
  34.9 11.8 %copy-start.3 = (s32[2048]{0:T(1024)S(1)}, s32[2048]{0:T(1024)}, u32[]{:S(2)}) copy-start(s32[2048]{0:T(1024)} %param.22) | copy-start | bytes 24580
  46.7 12.0 %copy-start.16 = (s32[16,12]{1,0:T(8,128)S(1)}, s32[16,12]{1,0:T(8,128)}, u32[]{:S(2)}) copy-start(s32[16,12]{1,0:T(8,128)} %param.16) | copy-start | bytes 2308
  67.7 33.2 %all-to-all-start.1 = ((s32[32,1,128]{2,1,0:T(1,128)}), s32[32,1,128]{2,1,0:T(1,128)S(1)}, u32[]{:S(2)}, u32[]{:S(2)}) async-start(s32[32,1,128]{2,1,0:T(1,128)} %reshape.253), calls=%async_computation.1 | async-start | bytes 32768 | tf_op jit(solution)/shard_map/all_to_all | solution.py:83
  78.1 7.4 %copy-start.5 = (bf16[2048,128]{1,0:T(8,128)(2,1)S(1)}, bf16[2048,128]{1,0:T(8,128)(2,1)}, u32[]{:S(2)}) copy-start(bf16[2048,128]{1,0:T(8,128)(2,1)} %get-tuple-element.13) | copy-start | bytes 1572868
  78.1 7.4 %copy-start.6 = (bf16[2048,128]{1,0:T(8,128)(2,1)S(1)}, bf16[2048,128]{1,0:T(8,128)(2,1)}, u32[]{:S(2)}) copy-start(bf16[2048,128]{1,0:T(8,128)(2,1)} %get-tuple-element.16) | copy-start | bytes 1572868
  84.7 0.8 copy-start.8
  101.0 6.8 %copy-start.9 = (bf16[256,172]{0,1:T(8,128)(2,1)S(1)}, bf16[256,172]{0,1:T(8,128)(2,1)}, u32[]{:S(2)}) copy-start(bf16[256,172]{0,1:T(8,128)(2,1)} %param.25) | copy-start | bytes 264196
  101.0 86.1 %all-to-all-start.2 = ((bf16[32,64,512]{2,1,0:T(8,128)(2,1)}), bf16[32,64,512]{2,1,0:T(8,128)(2,1)}, u32[]{:S(2)}, u32[]{:S(2)}) async-start(bf16[32,64,512]{2,1,0:T(8,128)(2,1)} %broadcast_select_fusion), calls=%async_computation.2 | async-start | bytes 4194304 | tf_op jit(solution)/shard_map/all_to_all | solution.py:82
  106.9 80.1 %all-gather.2.cloned.1.call-start = ((), (), s32[]{:S(2)}) async-start(), calls=%async_computation.6 | async-start | bytes 1310720 | tf_op jit(solution)/shard_map/all_gather | solution.py:87
  107.7 121.3 %reduce-scatter.8.cloned.1.call-start = ((), (), s32[]{:S(2)}) async-start(), calls=%async_computation.9 | async-start | bytes 901120 | tf_op jit(solution)/shard_map/reduce_scatter | solution.py:104
  191.3 3.9 %copy-start.4 = (f32[2048,1024]{1,0:T(8,128)}, f32[2048,1024]{1,0:T(8,128)S(1)}, u32[]{:S(2)}) copy-start(f32[2048,1024]{1,0:T(8,128)S(1)} %get-tuple-element.20) | copy-start | bytes 25165828
  191.3 1.3 copy-start.7
  192.6 1.6 copy-start.12
  192.6 3.2 copy-start.17
  195.2 0.6 copy-start.13
  205.7 68.2 %reduce-scatter.4.cloned.1.call-start = ((), (), s32[]{:S(2)}) async-start(), calls=%async_computation.7 | async-start | bytes 2621440 | tf_op jit(solution)/shard_map/reduce_scatter | solution.py:103
  217.1 56.9 %copy-start.14 = (f32[2048]{0:T(1024)S(1)}, f32[2048]{0:T(1024)}, u32[]{:S(2)}) copy-start(f32[2048]{0:T(1024)} %copy-done.13) | copy-start | bytes 24580
  217.1 56.9 %copy-start.15 = (f32[2048]{0:T(1024)S(1)}, f32[2048]{0:T(1024)}, u32[]{:S(2)}) copy-start(f32[2048]{0:T(1024)} %get-tuple-element.8) | copy-start | bytes 24580
  217.1 57.0 %copy-start.11 = (f32[1,32,64]{2,0,1:T(1,128)S(1)}, f32[1,32,64]{2,0,1:T(1,128)}, u32[]{:S(2)}) copy-start(f32[1,32,64]{2,0,1:T(1,128)} %get-tuple-element.18) | copy-start | bytes 24580
  217.1 57.1 %copy-start.19 = (f32[32]{0:T(128)S(1)}, f32[32]{0:T(128)}, u32[]{:S(2)}) copy-start(f32[32]{0:T(128)} %get-tuple-element.10) | copy-start | bytes 388
  217.1 112.0 %all-reduce.2.cloned.1.call-start = ((), (), s32[]{:S(2)}) async-start(), calls=%async_computation.10 | async-start | bytes 360448 | tf_op jit(solution)/shard_map/psum | solution.py:107
  229.0 137.9 %reduce-scatter.6.cloned.1.call-start = ((), (), s32[]{:S(2)}) async-start(), calls=%async_computation.8 | async-start | bytes 589824 | tf_op jit(solution)/shard_map/reduce_scatter | solution.py:106
Sparse Core Ops, SparseCore 0:
  109.3 55.8 all-gather.1
  205.8 23.0 reduce-scatter.7
  231.2 42.6 reduce-scatter.3
  276.9 52.1 all-reduce.1
  332.6 34.2 reduce-scatter.5
where the time goes:
time: 376 us; the launch traced here: 375 us
  waiting for transfers between devices  150 us (40%)
  blocking collectives  73.9 us (20%)
  local copies, waits for them, and re-layouts  68.5 us (18%)
  matrix products  35.3 us (9%)
  starting transfers between devices  19.3 us (5%)
  between operations  14.8 us (4%)
  other arithmetic  13.5 us (4%)
    all_gather x1, blocking collectives, shards(): lax.all_gather(w_second, 'rep', axis=0, tiled=True)  73.9 us
    psum x1, waiting for transfers between devices, shards(): grad_two = lax.psum(grad_two_rep, 'dom')  54.4 us
    reduce_scatter x1, waiting for transfers between devices, shards(): lax.psum_scatter(grad_one_full, 'rep', scatter_dimension=1, tiled=True)  44.9 us
    reduce_scatter x1, waiting for transfers between devices, shards(): lax.psum_scatter(grad_one_rep, 'dom', scatter_dimension=0, tiled=True)  37.7 us
    dot_general x2, matrix products, contract_rows(): lax.dot_general(left, right, (((0,), (0,)), ((), ())), preferred_element_...  13.2 us
    gather x1, local copies, waits for them, and re-layouts, shards(): order = jnp.take(train_ids[0], shuffle[0], axis=0)  11.8 us
    gather x1, local copies, waits for them, and re-layouts, shards(): own_labels = jnp.take(labels, order, axis=0)  11.8 us
    gather x1, local copies, waits for them, and re-layouts, shards(): own_marks = jnp.take(labelled, order, axis=0)  11.8 us
  transfers between devices with their start and end apart: 8, of which 4 were waited for; matrix products, arithmetic and copies ran while one was open for 23% of the time, Pallas kernels for 0%

commit v1 on v0

v1 whole, which is shorter than its diff:
```python
import functools

import jax
import jax.numpy as jnp
from jax import lax
from jax.experimental import pallas as pl
from jax.experimental.pallas import tpu as pltpu
from jax.sharding import PartitionSpec as P

F32 = jnp.float32
BF16 = jnp.bfloat16
BIG = 60 * 1024 * 1024


def where_am_i(ndom, nrep):
    return lax.axis_index("dom") * nrep + lax.axis_index("rep")


def enter(me, n, nrep):
    barrier = pltpu.get_barrier_semaphore()

    def greet(o, carry):
        peer = lax.rem(me + o, n)
        pl.semaphore_signal(barrier, inc=1, device_id=(peer // nrep, lax.rem(peer, nrep)),
                            device_id_type=pl.DeviceIdType.MESH)
        return carry

    lax.fori_loop(1, n, greet, 0)
    pl.semaphore_wait(barrier, n - 1)


def spread(me, n, nrep, src_at, dst, send_sem, recv_sem):
    def copy(o):
        peer = lax.rem(me + o, n)
        return pltpu.make_async_remote_copy(
            src_ref=src_at(peer), dst_ref=dst.at[me],
            send_sem=send_sem.at[o], recv_sem=recv_sem.at[o],
            device_id=(peer // nrep, lax.rem(peer, nrep)),
            device_id_type=pl.DeviceIdType.MESH)

    def start(o, carry):
        copy(o).start()
        return carry

    def finish(o, carry):
        copy(o).wait()
        return carry

    return (lambda: lax.fori_loop(1, n, start, 0)), (lambda: lax.fori_loop(1, n, finish, 0))


def comm_call(kernel, outs, scratch, name, cid, *args):
    return pl.pallas_call(
        kernel,
        out_shape=outs,
        in_specs=[pl.BlockSpec(memory_space=pltpu.VMEM)] * len(args),
        out_specs=jax.tree.map(lambda _: pl.BlockSpec(memory_space=pltpu.VMEM), outs),
        scratch_shapes=scratch,
        compiler_params=pltpu.CompilerParams(collective_id=cid, has_side_effects=True),
        name=name,
    )(*args)


def dma_sems(n, count):
    return [pltpu.SemaphoreType.DMA((n,))] * count


def halo_kernel(ndom, nrep, src, out, buf, ssem, rsem):
    n = ndom * nrep
    me = where_am_i(ndom, nrep)
    enter(me, n, nrep)
    start, finish = spread(me, n, nrep, lambda p: src.at[p], buf, ssem, rsem)
    start()
    buf[me] = src[me]
    finish()
    out[...] = buf[...]


def stats_kernel(ndom, nrep, forward, chunk, src, out, extra, recv, gath, s1, r1, s2, r2):
    n = ndom * nrep
    me = where_am_i(ndom, nrep)
    enter(me, n, nrep)
    start, finish = spread(me, n, nrep, lambda p: src.at[p], recv, s1, r1)
    start()
    recv[me] = src[me]
    finish()
    third = src.shape[1] // 3
    got = recv[...]
    first = jnp.sum(got[:, :third], axis=0)
    second = jnp.sum(got[:, third:2 * third], axis=0)
    if forward:
        mu = first * (1.0 / n)
        off = got[:, :third] - mu[None]
        m2 = second + chunk * jnp.sum(off * off, axis=0)
        rstd = lax.rsqrt(m2 * (1.0 / (n * chunk)) + 1e-05)
        count = jnp.maximum(jnp.sum(got[:, 2 * third:], axis=0), 1.0)
        result = jnp.concatenate([mu, rstd, count], axis=0)
        extra[...] = jnp.zeros_like(extra)
    else:
        scale = 1.0 / (n * chunk)
        result = jnp.concatenate([first * scale, second * scale], axis=0)
        extra[...] = got[:, 2 * third:2 * third + 8]
    gath[me] = result
    start, finish = spread(me, n, nrep, lambda p: gath.at[me], gath, s2, r2)
    start()
    finish()
    out[...] = gath[...]


def grads_kernel(ndom, nrep, split, src, out1, out2, recv, gath, s1, r1, s2, r2):
    n = ndom * nrep
    me = where_am_i(ndom, nrep)
    dom, rep = lax.axis_index("dom"), lax.axis_index("rep")
    enter(me, n, nrep)
    start, finish = spread(me, n, nrep, lambda p: src.at[p], recv, s1, r1)
    start()
    recv[me] = src[me]
    finish()

    def add(q, total):
        return total + recv[q].astype(F32)

    total = lax.fori_loop(1, n, add, recv[0].astype(F32))
    out1[...] = total[:split]
    gath[dom] = total[split:]

    def copy(o):
        peer = lax.rem(dom + o, ndom)
        return pltpu.make_async_remote_copy(
            src_ref=gath.at[dom], dst_ref=gath.at[dom],
            send_sem=s2.at[o], recv_sem=r2.at[o], device_id=(peer, rep),
            device_id_type=pl.DeviceIdType.MESH)

    for o in range(1, ndom):
        copy(o).start()
    for o in range(1, ndom):
        copy(o).wait()
    out2[...] = gath[...]


def hop_kernel(kl, kh, lcols, hcols, adj_l, adj_h, own, halo, out):
    i = pl.program_id(0)
    left = jnp.concatenate([adj_l[0, k] for k in range(kl)] + [adj_h[0, k] for k in range(kh)], axis=1)
    right = jnp.concatenate(
        [own[lcols[i, k]] for k in range(kl)] + [halo[hcols[i, k]] for k in range(kh)], axis=0)
    out[0] = jnp.dot(left, right, preferred_element_type=F32).astype(BF16)


def pre_kernel(chunk, shuf, ids, feats, hop, aux, w1, x_out, z_out, aux_out, st_out):
    rows = shuf.shape[0]
    slots = ids.shape[0]
    width = feats.shape[2]
    lanes = lax.broadcasted_iota(jnp.int32, (rows, slots), 1)
    pick = (lanes == shuf[...]).astype(F32).astype(BF16)
    two = jnp.dot(pick, ids[...], preferred_element_type=F32)
    order = (two[:, 0:1] * 256.0 + two[:, 1:2]).astype(jnp.int32)
    nodes = feats.shape[1]
    lanes = lax.broadcasted_iota(jnp.int32, (rows, nodes), 1)
    pick = (lanes == order).astype(F32).astype(BF16)
    whole = jnp.concatenate([feats[0], feats[1], feats[2], hop[...], aux[...]], axis=1)
    got = jnp.dot(pick, whole, preferred_element_type=F32)
    x = got[:, :4 * width].astype(BF16)
    x_out[...] = x
    tags = got[:, 4 * width:]
    aux_out[...] = tags
    z = jnp.concatenate(
        [jnp.dot(x, w1[r], preferred_element_type=F32) for r in range(w1.shape[0])], axis=1)
    z_out[...] = z
    groups = rows // chunk
    z3 = z.reshape(groups, chunk, z.shape[1])
    mean = jnp.sum(z3, axis=1, keepdims=True) * (1.0 / chunk)
    off = z3 - mean
    st_out[:, 0:1] = mean
    st_out[:, 1:2] = jnp.sum(off * off, axis=1, keepdims=True)
    count = jnp.sum(tags[:, 1:2].reshape(groups, chunk, 1), axis=1, keepdims=True)
    st_out[:, 2:3] = jnp.broadcast_to(count, mean.shape)


def head_kernel(chunk, z_ref, aux, st, w2, dl_out, g2_out, gs_out):
    rows, hidden_units = z_ref.shape
    groups = rows // chunk
    stats = st[...]
    z3 = z_ref[...].reshape(groups, chunk, hidden_units)
    normed = ((z3 - stats[:, 0:1]) * stats[:, 1:2]).reshape(rows, hidden_units)
    hidden = jnp.maximum(normed, 0.0).astype(BF16)
    second = w2[...]
    logits = jnp.dot(hidden, second, preferred_element_type=F32)
    row_max = jnp.max(logits, axis=1, keepdims=True)
    expos = jnp.exp(logits - row_max)
    totals = jnp.sum(expos, axis=1, keepdims=True)
    target = aux[:, 0:1].astype(jnp.int32)
    mark = aux[:, 1:2]
    onehot = (lax.broadcasted_iota(jnp.int32, logits.shape, 1) == target).astype(F32)
    cross = jnp.log(totals) + row_max - jnp.sum(onehot * logits, axis=1, keepdims=True)
    count = jnp.broadcast_to(stats[:, 2:3, 0:1], (groups, chunk, 1)).reshape(rows, 1)
    dlogits = ((expos / totals - onehot) * (mark / count)).astype(BF16)
    dl_out[...] = dlogits

    @pl.when(pl.program_id(0) == 0)
    def _():
        g2_out[...] = jnp.zeros_like(g2_out)

    g2_out[...] += lax.dot_general(hidden, dlogits, (((0,), (0,)), ((), ())), preferred_element_type=F32)
    back = lax.dot_general(dlogits, second, (((1,), (1,)), ((), ())), preferred_element_type=F32)
    masked = jnp.where(normed > 0, back, 0.0)
    gs_out[:, 0:1] = jnp.sum(masked.reshape(groups, chunk, hidden_units), axis=1, keepdims=True)
    gs_out[:, 1:2] = jnp.sum((masked * normed).reshape(groups, chunk, hidden_units), axis=1, keepdims=True)
    weighted = jnp.sum((mark * cross).reshape(groups, chunk, 1), axis=1, keepdims=True)
    own_count = jnp.sum(mark.reshape(groups, chunk, 1), axis=1, keepdims=True)
    loss = weighted / jnp.maximum(own_count, 1.0)
    gs_out[:, 2:3] = jnp.broadcast_to(loss, (groups, 1, hidden_units))


def tail_kernel(chunk, z_ref, x_ref, st, gm, w2, dl, g1_out):
    rows, hidden_units = z_ref.shape
    groups = rows // chunk
    stats = st[...]
    means = gm[...]
    z3 = z_ref[...].reshape(groups, chunk, hidden_units)
    rstd = stats[:, 1:2]
    normed = (z3 - stats[:, 0:1]) * rstd
    back = lax.dot_general(dl[...], w2[...], (((1,), (1,)), ((), ())), preferred_element_type=F32)
    masked = jnp.where(normed > 0, back.reshape(groups, chunk, hidden_units), 0.0)
    dpre = ((masked - means[:, 0:1] - normed * means[:, 1:2]) * rstd).reshape(rows, hidden_units)

    @pl.when(pl.program_id(0) == 0)
    def _():
        g1_out[...] = jnp.zeros_like(g1_out)

    g1_out[...] += lax.dot_general(
        x_ref[...], dpre.astype(BF16), (((0,), (0,)), ((), ())), preferred_element_type=F32)


def whole_spec(shape):
    return pl.BlockSpec(tuple(shape), lambda i: (0,) * len(shape))


def lead_spec(shape):
    return pl.BlockSpec(tuple(shape), lambda i: (i,) + (0,) * (len(shape) - 1))


def gather_rep(shard, nrep, rep):
    slots = jnp.zeros((nrep,) + shard.shape, shard.dtype)
    slots = lax.dynamic_update_slice(slots, shard[None], (rep, 0, 0))
    for o in range(1, nrep):
        moved = lax.ppermute(shard, "rep", [(s, (s + o) % nrep) for s in range(nrep)])
        slots = lax.dynamic_update_slice(slots, moved[None], (lax.rem(rep - o + nrep, nrep), 0, 0))
    return slots


def shards(hop_feats, adj_local, local_cols, adj_halo, halo_cols, boundary_rows, train_ids,
           shuffle, labels, labelled, w_first, w_second):
    ndom, nrep = lax.axis_size("dom"), lax.axis_size("rep")
    n = ndom * nrep
    rep = lax.axis_index("rep")
    row_tiles, kl, tile, _ = adj_local.shape
    kh = adj_halo.shape[1]
    rows, width = hop_feats.shape[1:]
    slots = train_ids.shape[1]
    hidden_units, classes = w_second.shape[0] * nrep, w_second.shape[1]
    chunk = slots // n
    block = 256
    steps = slots // block
    groups = block // chunk
    big = pltpu.CompilerParams(vmem_limit_bytes=BIG)
    sds = jax.ShapeDtypeStruct

    w1 = gather_rep(w_first, nrep, rep)
    w2 = gather_rep(w_second, nrep, rep).reshape(hidden_units, classes)

    hop_two = hop_feats[2]
    pick = (boundary_rows[0][:, None] == lax.broadcasted_iota(jnp.int32, (1, rows), 1)).astype(BF16)
    sent = jnp.dot(pick, hop_two, preferred_element_type=F32).astype(BF16)
    share = sent.shape[0] // n
    sent = sent.reshape(n, share, width)
    halo = comm_call(
        functools.partial(halo_kernel, ndom, nrep), sds(sent.shape, BF16),
        [pltpu.VMEM(sent.shape, BF16)] + dma_sems(n, 2), "halo", 1, sent)
    halo = halo.reshape(-1, tile, width)

    next_hop = pl.pallas_call(
        functools.partial(hop_kernel, kl, kh),
        out_shape=sds((row_tiles, tile, width), BF16),
        grid=(row_tiles,),
        in_specs=[
            pl.BlockSpec(memory_space=pltpu.SMEM), pl.BlockSpec(memory_space=pltpu.SMEM),
            lead_spec((1, kl, tile, tile)), lead_spec((1, kh, tile, tile)),
            whole_spec((row_tiles, tile, width)), whole_spec(halo.shape)],
        out_specs=lead_spec((1, tile, width)),
        compiler_params=big, name="hop",
    )(local_cols, halo_cols, adj_local, adj_halo, hop_two.reshape(row_tiles, tile, width), halo)
    next_hop = next_hop.reshape(rows, width)

    lane = lax.broadcasted_iota(jnp.int32, (1, 128), 1)
    ids = train_ids[0][:, None]
    ids = jnp.where(lane == 0, ids // 256, jnp.where(lane == 1, ids % 256, 0)).astype(F32).astype(BF16)
    aux = jnp.where(lane == 0, labels[:, None], jnp.where(lane == 1, labelled[:, None], 0))
    aux = aux.astype(F32).astype(BF16)
    x, z, tags, stats = pl.pallas_call(
        functools.partial(pre_kernel, chunk),
        out_shape=(sds((slots, 4 * width), BF16), sds((slots, hidden_units), F32),
                   sds((slots, 128), F32), sds((n, 3, hidden_units), F32)),
        grid=(steps,),
        in_specs=[lead_spec((block, 1)), whole_spec((slots, 128)), whole_spec(hop_feats.shape),
                  whole_spec((rows, width)), whole_spec((rows, 128)), whole_spec(w1.shape)],
        out_specs=(lead_spec((block, 4 * width)), lead_spec((block, hidden_units)),
                   lead_spec((block, 128)), lead_spec((groups, 3, hidden_units))),
        compiler_params=big, name="pre",
    )(shuffle[0][:, None], ids, hop_feats, next_hop, aux, w1)

    lines = 3 * hidden_units // 128
    third = lines // 3

    def combine(values, forward, cid):
        out_lines = lines if forward else 2 * third
        return comm_call(
            functools.partial(stats_kernel, ndom, nrep, forward, chunk),
            (sds((n, out_lines, 128), F32), sds((n, 8, 128), F32)),
            [pltpu.VMEM((n, lines, 128), F32), pltpu.VMEM((n, out_lines, 128), F32)] + dma_sems(n, 4),
            "stats_f" if forward else "stats_b", cid, values.reshape(n, lines, 128))

    stats, _ = combine(stats, True, 2)
    stats = stats.reshape(n, 3, hidden_units)

    dlogits, grad_two, gsums = pl.pallas_call(
        functools.partial(head_kernel, chunk),
        out_shape=(sds((slots, classes), BF16), sds((hidden_units, classes), F32),
                   sds((n, 3, hidden_units), F32)),
        grid=(steps,),
        in_specs=[lead_spec((block, hidden_units)), lead_spec((block, 128)),
                  lead_spec((groups, 3, hidden_units)), whole_spec((hidden_units, classes))],
        out_specs=(lead_spec((block, classes)), whole_spec((hidden_units, classes)),
                   lead_spec((groups, 3, hidden_units))),
        compiler_params=big, name="head",
    )(z, tags, stats, w2)

    gmeans, losses = combine(gsums, False, 3)
    gmeans = gmeans.reshape(n, 2, hidden_units)
    loss = losses[:, 0, 0].reshape(1, n)

    grad_one = pl.pallas_call(
        functools.partial(tail_kernel, chunk),
        out_shape=sds((4 * width, hidden_units), F32),
        grid=(steps,),
        in_specs=[lead_spec((block, hidden_units)), lead_spec((block, 4 * width)),
                  lead_spec((groups, 3, hidden_units)), lead_spec((groups, 2, hidden_units)),
                  whole_spec((hidden_units, classes)), lead_spec((block, classes))],
        out_specs=whole_spec((4 * width, hidden_units)),
        compiler_params=big, name="tail",
    )(z, x, stats, gmeans, w2, dlogits)

    own_rows, own_cols = 4 * width // ndom, hidden_units // nrep
    one = grad_one.astype(BF16).reshape(ndom, own_rows, nrep, own_cols).transpose(0, 2, 1, 3)
    one = one.reshape(n, own_rows, own_cols)
    part = hidden_units // n
    two = grad_two.astype(BF16).reshape(nrep, ndom, part, classes).transpose(1, 0, 2, 3)
    two = jnp.pad(two.reshape(n, part, classes), ((0, 0), (0, 0), (0, own_cols - classes)))
    packed = jnp.concatenate([one, two], axis=1)
    first, second = comm_call(
        functools.partial(grads_kernel, ndom, nrep, own_rows),
        (sds((own_rows, own_cols), F32), sds((ndom, part, own_cols), F32)),
        [pltpu.VMEM(packed.shape, BF16), pltpu.VMEM((ndom, part, own_cols), F32)] + dma_sems(n, 4),
        "grads", 4, packed)
    second = second.reshape(ndom * part, own_cols)[:, :classes]
    return (next_hop, loss, first, second)


def solution(mesh):
    both = ("dom", "rep")
    placed = (
        P(None, both, None), P(both, None, None, None), P(both, None), P(both, None, None, None),
        P(both, None), P(both, None), P(both, None), P(both, None), P(both), P(both),
        P(None, "rep"), P("rep", None),
    )
    return jax.shard_map(
        shards, mesh=mesh, in_specs=placed,
        out_specs=(P(both, None), P(both, None), P("dom", "rep"), P("rep", None)),
        check_vma=False,
    )
```

time: 376 us -> 223 us (0.59)
  Pallas kernels: 0 us -> 180 us
  waiting for transfers between devices: 150 us -> 2.26 us
  blocking collectives: 73.9 us -> 0 us
  local copies, waits for them, and re-layouts: 68.5 us -> 19.2 us
  matrix products: 35.3 us -> 2.61 us
  between operations: 14.8 us -> 0.96 us
  starting transfers between devices: 19.3 us -> 10.2 us
  other arithmetic: 13.5 us -> 7.08 us
    pallas_call x0 -> x8, Pallas kernels: none -> 180 us  [the longest x4 124 us: comm_call(): pl.pallas_call(kernel, out_shape=outs, in_specs=[pl.BlockSpec(memory_spac...]
    reduce_scatter x3 -> x0, waiting for transfers between devices: 94.5 us -> none  [the longest x1 44.9 us: shards(): lax.psum_scatter(grad_one_full, 'rep', scatter_dimension=1, tiled=True)]
    all_gather x1 -> x0, blocking collectives: 73.9 us -> none  [shards(): lax.all_gather(w_second, 'rep', axis=0, tiled=True)]
    gather x7 -> x0, local copies, waits for them, and re-layouts: 57.9 us -> none  [the longest x1 11.8 us: shards(): order = jnp.take(train_ids[0], shuffle[0], axis=0)]
    psum x1 -> x0, waiting for transfers between devices: 54.4 us -> none  [shards(): grad_two = lax.psum(grad_two_rep, 'dom')]
    dot_general x7 -> x1, matrix products: 35.3 us -> 2.61 us  [shards(): sent = jnp.dot(pick, hop_two, preferred_element_type=F32).astype(BF16)]
    all_to_all x3 -> x0, starting transfers between devices: 19.1 us -> none  [the longest x1 7.32 us: shards(): lax.all_to_all(sent, ('dom', 'rep'), split_axis=0, concat_axis=0, tiled=T...]
    ppermute x0 -> x6, starting transfers between devices: none -> 10.2 us  [gather_rep(): lax.ppermute(shard, 'rep', [(s, (s + o) % nrep) for s in range(nrep)])]
  transfers between devices with their start and end apart: 8 -> 6, of which waited for: 4 -> 1; matrix products, arithmetic and copies ran while one was open for 23% -> 5% of each run, Pallas kernels for 0% -> 17%
where the time goes in v1:
time: 223 us; the launch traced here: 222 us
  Pallas kernels  180 us (81%)
  local copies, waits for them, and re-layouts  19.2 us (9%)
  starting transfers between devices  10.2 us (5%)
  other arithmetic  7.08 us (3%)
  matrix products  2.61 us (1%)
  waiting for transfers between devices  2.26 us (1%)
    pallas_call x4, Pallas kernels, comm_call(): pl.pallas_call(kernel, out_shape=outs, in_specs=[pl.BlockSpec(memory_spac...  124 us
    pallas_call x1, Pallas kernels, shards(): pl.pallas_call(functools.partial(pre_kernel, chunk), out_shape=(sds((slot...  18.7 us
    pallas_call x1, Pallas kernels, shards(): pl.pallas_call(functools.partial(head_kernel, chunk), out_shape=(sds((slo...  12.7 us
    pallas_call x1, Pallas kernels, shards(): pl.pallas_call(functools.partial(hop_kernel, kl, kh), out_shape=sds((row_...  12.5 us
    pallas_call x1, Pallas kernels, shards(): pl.pallas_call(functools.partial(tail_kernel, chunk), out_shape=sds((4 *...  11.9 us
    ppermute x6, starting transfers between devices, gather_rep(): lax.ppermute(shard, 'rep', [(s, (s + o) % nrep) for s in range(nrep)])  10.2 us
    unnamed x21, local copies, waits for them, and re-layouts  5.66 us
  transfers between devices with their start and end apart: 6, of which 1 were waited for; matrix products, arithmetic and copies ran while one was open for 5% of the time, Pallas kernels for 17%

profile of v1, /device:TPU:0, one launch (start us, length us, event | category | flops | bytes accessed | tf_op | source)
XLA Modules:
  0.0 222.0 jit_solution(1452248639629531096)
XLA Ops:
  0.6 0.0 copy-start.5
  0.6 3.1 %collective-permute-start = (bf16[512,256]{1,0:T(8,128)(2,1)}, bf16[512,256]{1,0:T(8,128)(2,1)S(1)}, u32[]{:S(2)}, u32[]{:S(2)}) collective-permute-start(bf16[512,256]{1,0:T(8,128)(2,1)} %param.22), channel_id=1, source_target_pairs={{0,1},{1,2},{2,3},{3,0},{4,5},{5,6},{6,7},{7,4},{8,9},{9,10},{10,1... | collective-permute-start | bytes 786440 | tf_op jit(solution)/shard_map/ppermute | solution.py:246
  3.7 2.6 %collective-permute-start.1 = (bf16[512,256]{1,0:T(8,128)(2,1)}, bf16[512,256]{1,0:T(8,128)(2,1)S(1)}, u32[]{:S(2)}, u32[]{:S(2)}) collective-permute-start(bf16[512,256]{1,0:T(8,128)(2,1)} %param.22), channel_id=1, source_target_pairs={{0,2},{1,3},{2,0},{3,1},{4,6},{5,7},{6,4},{7,5},{8,10},{9,11},{10,... | collective-permute-start | bytes 786440 | tf_op jit(solution)/shard_map/ppermute | solution.py:246
  6.3 1.3 collective-permute-start.2
  7.7 0.7 collective-permute-start.3
  8.4 0.3 collective-permute-start.4
  8.7 1.4 copy.24.hcols
  10.1 1.9 slice.9
  11.9 2.6 %fusion.4 = bf16[512,128]{1,0:T(8,128)(2,1)} fusion(s32[512]{0:T(512)} %bitcast.51, bf16[3,2048,128]{2,1,0:T(8,128)(2,1)} %feats.1), kind=kOutput, calls=%fused_computation.6 | convolution fusion | flops 269549568 | bytes 657408 | tf_op jit(solution)/shard_map/dot_general | solution.py:273
  14.5 25.5 %halo.1 = bf16[32,16,128]{2,1,0:T(8,128)(2,1)} custom-call(bf16[32,16,128]{2,1,0:T(8,128)(2,1)} %bitcast.43), custom_call_target="tpu_custom_call" | custom-call | tf_op jit(solution)/shard_map/halo/pallas_call | solution.py:53
  40.1 0.0 copy-done.5
  40.1 1.4 copy.25.shuf
  41.5 0.1 copy.26
  41.6 0.1 broadcast_in_dim.96
  41.7 0.0 copy-start.6
  41.7 0.0 copy-start.7
  41.8 12.5 %hop.1 = bf16[16,128,128]{2,1,0:T(8,128)(2,1)} custom-call(s32[16,12]{1,0:T(8,128)} %lcols.1, s32[16,4]{1,0:T(8,128)} %copy.24.hcols, bf16[16,12,128,128]{3,2,1,0:T(8,128)(2,1)} %adj_l.1, bf16[16,4,128,128]{3,2,1,0:T(8,128)(2,1)} %adj_h.1, bf16[16,128,128]{2,1,0:T(8,128)(2,1)} %bitcast.38, bf16[4,128,128]{2,1,0:T(8,128)(2,1)} %bitcast.41), custom_call_target="tpu_custom_call" | custom-call | tf_op jit(solution)/shard_map/hop/pallas_call | solution.py:281
  54.2 2.7 %convert_convert_fusion = (bf16[2048,128]{1,0:T(8,128)(2,1)}, bf16[2048,128]{1,0:T(8,128)(2,1)}) fusion(s32[2048]{0:T(1024)S(1)} %copy-done.6, s32[2048]{0:T(1024)S(1)} %copy-done.7, pred[128]{0:T(512)(128)(4,1)S(1)} %get-tuple-element.32, pred[128]{0:T(512)(128)(4,1)S(1)} %get-tuple-element.33, s32[2048]{0:T(1024)S(1)} %get-tuple-element.29, ...), kind=kLoop, calls=%fused_computation.7 | loop fusion | flops 2097152 | bytes 1081600 | tf_op jit(solution)/shard_map/convert_element_type | solution.py:298
  57.0 0.0 collective-permute-done.3
  57.0 2.2 collective-permute-start.5
  59.1 0.1 copy.27
  59.3 0.0 collective-permute-done.4
  59.3 0.1 copy.28
  59.4 2.2 %collective-permute-done.5 = bf16[256,172]{0,1:T(8,128)(2,1)S(1)} collective-permute-done((bf16[256,172]{0,1:T(8,128)(2,1)S(1)}, bf16[256,172]{0,1:T(8,128)(2,1)S(1)}, u32[]{:S(2)}, u32[]{:S(2)}) %collective-permute-start.5) | collective-permute-done | bytes 88096 | tf_op jit(solution)/shard_map/ppermute | solution.py:246
  61.6 0.1 copy.29
  61.8 0.0 collective-permute-done
  61.8 0.0 collective-permute-done.1
  61.9 0.0 collective-permute-done.2
  61.9 0.0 copy-start.1
  61.9 1.1 copy-done.1
  63.0 18.7 %pre.1 = (bf16[2048,512]{1,0:T(8,128)(2,1)}, f32[2048,1024]{1,0:T(8,128)}, f32[2048,128]{1,0:T(8,128)}, f32[32,3,1024]{2,1,0:T(4,128)}) custom-call(s32[2048,1]{1,0:T(8,128)} %copy.25.shuf, bf16[2048,128]{1,0:T(8,128)(2,1)} %get-tuple-element.31.ids, bf16[3,2048,128]{2,1,0:T(8,128)(2,1)} %feats.1, bf16[2048,128]{1,0:T(8,128)(2,1)} %bitcast.36, ...), custom_call_target="tpu_custom_call" | custom-call | tf_op jit(solution)/shard_map/pre/pallas_call | solution.py:299
  81.7 2.0 reshape.150.src
  83.7 28.7 %stats_f.1 = (f32[32,24,128]{2,1,0:T(8,128)}, f32[32,8,128]{2,1,0:T(8,128)}) custom-call(f32[32,24,128]{2,1,0:T(8,128)} %reshape.150.src), custom_call_target="tpu_custom_call" | custom-call | tf_op jit(solution)/shard_map/stats_f/pallas_call | solution.py:53
  112.4 2.0 reshape.151.st
  114.3 12.7 %head.1 = (bf16[2048,172]{1,0:T(8,128)(2,1)}, f32[1024,172]{1,0:T(8,128)}, f32[32,3,1024]{2,1,0:T(4,128)}) custom-call(f32[2048,1024]{1,0:T(8,128)} %get-tuple-element.16.z_ref, f32[2048,128]{1,0:T(8,128)} %get-tuple-element.17.aux, f32[32,3,1024]{2,1,0:T(4,128)} %reshape.151.st, bf16[1024,172]{1,0:T(8,128)(2,1)} %bitcast.33), custom_call_target="tpu_custom_call" | custom-call | tf_op jit(solution)/shard_map/head/pallas_call | solution.py:325
  127.1 2.0 reshape.153.src
  129.1 24.5 %stats_b.1 = (f32[32,16,128]{2,1,0:T(8,128)}, f32[32,8,128]{2,1,0:T(8,128)}) custom-call(f32[32,24,128]{2,1,0:T(8,128)} %reshape.153.src), custom_call_target="tpu_custom_call" | custom-call | tf_op jit(solution)/shard_map/stats_b/pallas_call | solution.py:53
  153.6 1.8 slice_reduce_fusion
  155.4 1.3 convert_element_type.30
  156.7 0.8 reshape.154.gm
  157.5 11.9 %tail.1 = f32[512,1024]{1,0:T(8,128)} custom-call(f32[2048,1024]{1,0:T(8,128)} %get-tuple-element.16.z_ref, bf16[2048,512]{1,0:T(8,128)(2,1)} %get-tuple-element.22.x_ref, f32[32,3,1024]{2,1,0:T(4,128)} %reshape.151.st, f32[32,2,1024]{2,1,0:T(2,128)} %reshape.154.gm, bf16[1024,172]{1,0:T(8,128)(2,1)} %bitcast.34, bf16[2048,172]{1,0:T(8,128)(2,1)} %get-tuple-element.24.dl), custom_call_target="tpu_custom_call" | custom-call | tf_op jit(solution)/shard_map/tail/pallas_call | solution.py:341
  169.5 1.7 convert_element_type.29
  171.2 0.8 reshape.155
  172.0 0.2 copy.30
  172.2 1.4 fusion.3.src
  173.6 45.2 %grads.1 = (f32[64,256]{1,0:T(8,128)}, f32[8,32,256]{2,1,0:T(8,128)}) custom-call(bf16[32,96,256]{2,1,0:T(8,128)(2,1)} %fusion.3.src), custom_call_target="tpu_custom_call" | custom-call | tf_op jit(solution)/shard_map/grads/pallas_call | solution.py:53
  218.8 1.7 copy.33
  220.6 1.5 copy.43
  (24 shorter events, 0.3 us)
Async XLA Ops:
  0.6 39.4 %copy-start.5 = (s32[1,2048]{1,0:T(1,128)S(1)}, s32[1,2048]{1,0:T(1,128)}, u32[]{:S(2)}) copy-start(s32[1,2048]{1,0:T(1,128)} %param.19) | copy-start | bytes 24580
  0.6 61.2 %collective-permute-start = (bf16[512,256]{1,0:T(8,128)(2,1)}, bf16[512,256]{1,0:T(8,128)(2,1)S(1)}, u32[]{:S(2)}, u32[]{:S(2)}) collective-permute-start(bf16[512,256]{1,0:T(8,128)(2,1)} %param.22), channel_id=1, source_target_pairs={{0,1},{1,2},{2,3},{3,0},{4,5},{5,6},{6,7},{7,4},{8,9},{9,10},{10,1... | collective-permute-start | bytes 786440 | tf_op jit(solution)/shard_map/ppermute | solution.py:246
  3.7 58.1 %collective-permute-start.1 = (bf16[512,256]{1,0:T(8,128)(2,1)}, bf16[512,256]{1,0:T(8,128)(2,1)S(1)}, u32[]{:S(2)}, u32[]{:S(2)}) collective-permute-start(bf16[512,256]{1,0:T(8,128)(2,1)} %param.22), channel_id=1, source_target_pairs={{0,2},{1,3},{2,0},{3,1},{4,6},{5,7},{6,4},{7,5},{8,10},{9,11},{10,... | collective-permute-start | bytes 786440 | tf_op jit(solution)/shard_map/ppermute | solution.py:246
  6.3 55.5 %collective-permute-start.2 = (bf16[512,256]{1,0:T(8,128)(2,1)}, bf16[512,256]{1,0:T(8,128)(2,1)S(1)}, u32[]{:S(2)}, u32[]{:S(2)}) collective-permute-start(bf16[512,256]{1,0:T(8,128)(2,1)} %param.22), channel_id=1, source_target_pairs={{0,3},{1,0},{2,1},{3,2},{4,7},{5,4},{6,5},{7,6},{8,11},{9,8},{10,9... | collective-permute-start | bytes 786440 | tf_op jit(solution)/shard_map/ppermute | solution.py:246
  7.7 49.3 %collective-permute-start.3 = (bf16[256,172]{0,1:T(8,128)(2,1)}, bf16[256,172]{0,1:T(8,128)(2,1)S(1)}, u32[]{:S(2)}, u32[]{:S(2)}) collective-permute-start(bf16[256,172]{0,1:T(8,128)(2,1)} %param.23), channel_id=1, source_target_pairs={{0,1},{1,2},{2,3},{3,0},{4,5},{5,6},{6,7},{7,4},{8,9},{9,10},{10,1... | collective-permute-start | bytes 264200 | tf_op jit(solution)/shard_map/ppermute | solution.py:246
  8.4 50.9 %collective-permute-start.4 = (bf16[256,172]{0,1:T(8,128)(2,1)}, bf16[256,172]{0,1:T(8,128)(2,1)S(1)}, u32[]{:S(2)}, u32[]{:S(2)}) collective-permute-start(bf16[256,172]{0,1:T(8,128)(2,1)} %param.23), channel_id=1, source_target_pairs={{0,2},{1,3},{2,0},{3,1},{4,6},{5,7},{6,4},{7,5},{8,10},{9,11},{10,... | collective-permute-start | bytes 264200 | tf_op jit(solution)/shard_map/ppermute | solution.py:246
  11.9 29.5 %copy-start.8 = (s32[1,2048]{1,0:T(1,128)S(1)}, s32[1,2048]{1,0:T(1,128)}, u32[]{:S(2)}) copy-start(s32[1,2048]{1,0:T(1,128)} %param.18) | copy-start | bytes 24580
  11.9 29.6 %copy-start.4 = (bf16[256,172]{0,1:T(8,128)(2,1)S(1)}, bf16[256,172]{0,1:T(8,128)(2,1)}, u32[]{:S(2)}) copy-start(bf16[256,172]{0,1:T(8,128)(2,1)} %param.23) | copy-start | bytes 264196
  11.9 29.7 %copy-start.2 = (bf16[512,256]{1,0:T(8,128)(2,1)S(1)}, bf16[512,256]{1,0:T(8,128)(2,1)}, u32[]{:S(2)}) copy-start(bf16[512,256]{1,0:T(8,128)(2,1)} %param.22) | copy-start | bytes 786436
  41.7 12.5 %copy-start.6 = (s32[2048]{0:T(1024)S(1)}, s32[2048]{0:T(1024)}, u32[]{:S(2)}) copy-start(s32[2048]{0:T(1024)} %param.21) | copy-start | bytes 24580
  41.7 12.5 %copy-start.7 = (s32[2048]{0:T(1024)S(1)}, s32[2048]{0:T(1024)}, u32[]{:S(2)}) copy-start(s32[2048]{0:T(1024)} %param.20) | copy-start | bytes 24580
  57.0 4.7 %collective-permute-start.5 = (bf16[256,172]{0,1:T(8,128)(2,1)S(1)}, bf16[256,172]{0,1:T(8,128)(2,1)S(1)}, u32[]{:S(2)}, u32[]{:S(2)}) collective-permute-start(bf16[256,172]{0,1:T(8,128)(2,1)S(1)} %copy-done.4), channel_id=1, source_target_pairs={{0,3},{1,0},{2,1},{3,2},{4,7},{5,4},{6,5},{7,6},{8,11},{9,8},{10,9... | collective-permute-start | bytes 264200 | tf_op jit(solution)/shard_map/ppermute | solution.py:246
  61.8 19.9 %copy-start = (bf16[4,256,172]{2,1,0:T(8,128)(2,1)}, bf16[4,256,172]{2,1,0:T(8,128)(2,1)S(1)}, u32[]{:S(2)}) copy-start(bf16[4,256,172]{2,1,0:T(8,128)(2,1)S(1)} %constant_dynamic-update-slice_fusion) | copy-start | bytes 1056772
  61.9 1.1 copy-start.1
  153.6 3.1 %copy-start.3 = (f32[32,16,128]{2,1,0:T(8,128)S(1)}, f32[32,16,128]{2,1,0:T(8,128)}, u32[]{:S(2)}) copy-start(f32[32,16,128]{2,1,0:T(8,128)} %get-tuple-element.23) | copy-start | bytes 786436

commit v2 on v1

v2 whole, which is shorter than its diff:
```python
import functools

import jax
import jax.numpy as jnp
from jax import lax
from jax.experimental import pallas as pl
from jax.experimental.pallas import tpu as pltpu
from jax.sharding import PartitionSpec as P

F32 = jnp.float32
BF16 = jnp.bfloat16
BIG = 60 * 1024 * 1024


def where_am_i(ndom, nrep):
    return lax.axis_index("dom") * nrep + lax.axis_index("rep")


def enter(me, n, nrep):
    barrier = pltpu.get_barrier_semaphore()

    def greet(o, carry):
        peer = lax.rem(me + o, n)
        pl.semaphore_signal(barrier, inc=1, device_id=(peer // nrep, lax.rem(peer, nrep)),
                            device_id_type=pl.DeviceIdType.MESH)
        return carry

    lax.fori_loop(1, n, greet, 0)
    pl.semaphore_wait(barrier, n - 1)


def spread(me, n, nrep, src_at, dst, send_sem, recv_sem):
    def copy(o):
        peer = lax.rem(me + o, n)
        return pltpu.make_async_remote_copy(
            src_ref=src_at(peer), dst_ref=dst.at[me],
            send_sem=send_sem.at[o], recv_sem=recv_sem.at[o],
            device_id=(peer // nrep, lax.rem(peer, nrep)),
            device_id_type=pl.DeviceIdType.MESH)

    def start(o, carry):
        copy(o).start()
        return carry

    def finish(o, carry):
        copy(o).wait()
        return carry

    return (lambda: lax.fori_loop(1, n, start, 0)), (lambda: lax.fori_loop(1, n, finish, 0))


def comm_call(kernel, outs, scratch, name, cid, *args):
    return pl.pallas_call(
        kernel,
        out_shape=outs,
        in_specs=[pl.BlockSpec(memory_space=pltpu.VMEM)] * len(args),
        out_specs=jax.tree.map(lambda _: pl.BlockSpec(memory_space=pltpu.VMEM), outs),
        scratch_shapes=scratch,
        compiler_params=pltpu.CompilerParams(collective_id=cid, has_side_effects=True),
        name=name,
    )(*args)


def dma_sems(n, count):
    return [pltpu.SemaphoreType.DMA((n,))] * count


def halo_kernel(ndom, nrep, src, cnt, out, tot, buf, crow, cbuf, ssem, rsem, s2, r2):
    n = ndom * nrep
    me = where_am_i(ndom, nrep)
    crow[0] = cnt[...]
    enter(me, n, nrep)
    start, finish = spread(me, n, nrep, lambda p: src.at[p], buf, ssem, rsem)
    cstart, cfinish = spread(me, n, nrep, lambda p: crow.at[0], cbuf, s2, r2)
    start()
    cstart()
    buf[me] = src[me]
    cbuf[me] = cnt[...]
    finish()
    cfinish()
    out[...] = buf[...]
    tot[...] = jnp.maximum(jnp.sum(cbuf[...], axis=0), 1.0)


def stats_kernel(ndom, nrep, forward, chunk, src, row, out, turned, recv, gath, lrow, lbuf,
                 s1, r1, s2, r2, s3, r3):
    n = ndom * nrep
    me = where_am_i(ndom, nrep)
    if not forward:
        lrow[0] = row[...]
    enter(me, n, nrep)
    start, finish = spread(me, n, nrep, lambda p: src.at[p], recv, s1, r1)
    start()
    lstart, lfinish = spread(me, n, nrep, lambda p: lrow.at[0], lbuf, s3, r3)
    if not forward:
        lstart()
        lbuf[me] = row[...]
    recv[me] = src[me]
    finish()
    half = src.shape[1] // 2
    got = recv[...]
    first = jnp.sum(got[:, :half], axis=0)
    second = jnp.sum(got[:, half:], axis=0)
    scale = 1.0 / (n * chunk)
    if forward:
        mu = first * (1.0 / n)
        off = got[:, :half] - mu[None]
        m2 = second + chunk * jnp.sum(off * off, axis=0)
        result = jnp.concatenate([mu, lax.rsqrt(m2 * scale + 1e-05)], axis=0)
    else:
        result = jnp.concatenate([first * scale, second * scale], axis=0)
    gath[me] = result
    start, finish = spread(me, n, nrep, lambda p: gath.at[me], gath, s2, r2)
    start()
    if forward:
        turned[...] = jnp.zeros_like(turned)
    else:
        lfinish()
        losses = lbuf[...]
        source = lax.broadcasted_iota(jnp.int32, losses.shape, 0)
        lane = lax.broadcasted_iota(jnp.int32, losses.shape, 2)
        mine = jnp.sum(jnp.where(lane == me, losses, 0.0), axis=2, keepdims=True)
        turned[...] = jnp.sum(jnp.where(lane == source, mine, 0.0), axis=0)
    finish()
    out[...] = gath[...]


def grads_kernel(ndom, nrep, cores, split, src, out1, out2, recv0, sum0, recv1, sum1, recv2, gath,
                 s0, r0, s1, r1, s2, r2, s3, r3):
    dom, rep = lax.axis_index("dom"), lax.axis_index("rep")
    me = dom * nrep + rep
    chips = ndom // cores
    chip, core = dom // cores, lax.rem(dom, cores)
    enter(me, ndom * nrep, nrep)

    def to(src_ref, dst_ref, ssem, rsem, peer_dom, peer_rep):
        return pltpu.make_async_remote_copy(
            src_ref=src_ref, dst_ref=dst_ref, send_sem=ssem, recv_sem=rsem,
            device_id=(peer_dom, peer_rep), device_id_type=pl.DeviceIdType.MESH)

    def run(copies):
        for copy in copies:
            copy.start()
        for copy in copies:
            copy.wait()

    other = cores - 1 - core
    run([to(src.at[other, a], recv0.at[a], s0.at[a], r0.at[a], chip * cores + other, rep)
         for a in range(chips)])
    sum0[...] = (src[core].astype(F32) + recv0[...].astype(F32)).astype(BF16)

    def near(o):
        peer = lax.rem(chip + o, chips)
        return to(sum0.at[peer], recv1.at[o - 1], s1.at[o], r1.at[o], peer * cores + core, rep)

    run([near(o) for o in range(1, chips)])
    total = sum0[chip].astype(F32)
    for o in range(1, chips):
        total = total + recv1[o - 1].astype(F32)
    sum1[...] = total.astype(BF16)

    def along(o):
        peer = lax.rem(rep + o, nrep)
        return to(sum1.at[peer], recv2.at[o - 1], s2.at[o], r2.at[o], dom, peer)

    run([along(o) for o in range(1, nrep)])
    total = sum1[rep].astype(F32)
    for o in range(1, nrep):
        total = total + recv2[o - 1].astype(F32)
    out1[...] = total[:split]
    gath[dom] = total[split:]
    run([to(gath.at[dom], gath.at[dom], s3.at[o], r3.at[o], lax.rem(dom + o, ndom), rep)
         for o in range(1, ndom)])
    out2[...] = gath[...]


def hop_kernel(kl, kh, lcols, hcols, adj_l, adj_h, own, halo, out):
    i = pl.program_id(0)
    left = jnp.concatenate([adj_l[0, k] for k in range(kl)] + [adj_h[0, k] for k in range(kh)], axis=1)
    right = jnp.concatenate(
        [own[0, lcols[i, k]] for k in range(kl)] + [halo[hcols[i, k]] for k in range(kh)], axis=0)
    out[0] = jnp.dot(left, right, preferred_element_type=F32).astype(BF16)


def batch_lanes(rows, wide, chunk):
    at = pl.program_id(0) * rows + lax.broadcasted_iota(jnp.int32, (rows, wide), 0)
    return at // chunk == lax.broadcasted_iota(jnp.int32, (rows, wide), 1)


def one_hot(column, count):
    lanes = lax.broadcasted_iota(jnp.int32, (column.shape[0], count), 1)
    return (lanes == column).astype(F32).astype(BF16)


def by_lanes(left, right):
    return lax.dot_general(left, right, (((1,), (1,)), ((), ())), preferred_element_type=F32)


def pick_kernel(chunk, shuf, bound, ids, labels, labelled, feats, x_out, tag_out, sent_out, cnt_out):
    rows = shuf.shape[0]
    nodes = feats.shape[1]
    sent_out[...] = jnp.dot(one_hot(bound[...], nodes), feats[2], preferred_element_type=F32).astype(BF16)
    numbers = ids[...]
    blank = jnp.zeros((6, nodes), F32)
    table = jnp.concatenate(
        [(numbers // 256).astype(F32), (numbers % 256).astype(F32), jnp.zeros((6, ids.shape[1]), F32)], axis=0)
    two = by_lanes(one_hot(shuf[...], ids.shape[1]), table.astype(BF16))
    order = two[:, 0:1] * 256.0 + two[:, 1:2]
    pick = one_hot(order.astype(jnp.int32), nodes)
    whole = jnp.concatenate([feats[0], feats[1], feats[2]], axis=1)
    x_out[...] = jnp.dot(pick, whole, preferred_element_type=F32).astype(BF16)
    marks = jnp.concatenate([labels[...].astype(F32), labelled[...].astype(F32), blank], axis=0)
    tags = by_lanes(pick, marks.astype(BF16))
    tag_out[:, 0:8] = tags
    tag_out[:, 8:9] = order

    @pl.when(pl.program_id(0) == 0)
    def _():
        cnt_out[...] = jnp.zeros_like(cnt_out)

    here = batch_lanes(rows, cnt_out.shape[1], chunk)
    cnt_out[...] += jnp.sum(jnp.where(here, tags[:, 1:2], 0.0), axis=0, keepdims=True)


def store_lines(out, at, value):
    for j in range(value.shape[2] // 128):
        out[:, at + j:at + j + 1] = value[:, :, j * 128:(j + 1) * 128]


def load_lines(ref, at, lines):
    return jnp.concatenate([ref[:, at + j:at + j + 1] for j in range(lines)], axis=2)


def pre_kernel(chunk, x3, tag, hop, w1, x_out, z_out, st_out):
    rows = x3.shape[0]
    order = tag[:, 8:9].astype(jnp.int32)
    got = jnp.dot(one_hot(order, hop.shape[0]), hop[...], preferred_element_type=F32)
    x = jnp.concatenate([x3[...], got.astype(BF16)], axis=1)
    x_out[...] = x
    z = jnp.concatenate(
        [jnp.dot(x, w1[r], preferred_element_type=F32) for r in range(w1.shape[0])], axis=1)
    z_out[...] = z
    z3 = z.reshape(rows // chunk, chunk, z.shape[1])
    mean = jnp.sum(z3, axis=1, keepdims=True) * (1.0 / chunk)
    off = z3 - mean
    store_lines(st_out, 0, mean)
    store_lines(st_out, st_out.shape[1] // 2, jnp.sum(off * off, axis=1, keepdims=True))


def head_kernel(chunk, z_ref, tag, st, counts, own_counts, w2, dl_out, g2_out, gs_out, loss_out):
    rows, hidden_units = z_ref.shape
    groups = rows // chunk
    half = st.shape[1] // 2
    z3 = z_ref[...].reshape(groups, chunk, hidden_units)
    normed = ((z3 - load_lines(st, 0, half)) * load_lines(st, half, half)).reshape(rows, hidden_units)
    hidden = jnp.maximum(normed, 0.0).astype(BF16)
    second = w2[...]
    logits = jnp.dot(hidden, second, preferred_element_type=F32)
    row_max = jnp.max(logits, axis=1, keepdims=True)
    expos = jnp.exp(logits - row_max)
    totals = jnp.sum(expos, axis=1, keepdims=True)
    target = tag[:, 0:1].astype(jnp.int32)
    mark = tag[:, 1:2]
    onehot = (lax.broadcasted_iota(jnp.int32, logits.shape, 1) == target).astype(F32)
    cross = jnp.log(totals) + row_max - jnp.sum(onehot * logits, axis=1, keepdims=True)
    here = batch_lanes(rows, counts.shape[1], chunk)
    count = jnp.sum(jnp.where(here, counts[...], 0.0), axis=1, keepdims=True)
    dlogits = ((expos / totals - onehot) * (mark / count)).astype(BF16)
    dl_out[...] = dlogits

    @pl.when(pl.program_id(0) == 0)
    def _():
        g2_out[...] = jnp.zeros_like(g2_out)
        loss_out[...] = jnp.zeros_like(loss_out)

    loss_out[...] += jnp.sum(jnp.where(here, mark * cross, 0.0), axis=0, keepdims=True)

    @pl.when(pl.program_id(0) == pl.num_programs(0) - 1)
    def _():
        loss_out[...] = loss_out[...] / jnp.maximum(own_counts[...], 1.0)

    g2_out[...] += lax.dot_general(hidden, dlogits, (((0,), (0,)), ((), ())), preferred_element_type=F32)
    masked = jnp.where(normed > 0, by_lanes(dlogits, second), 0.0)
    store_lines(gs_out, 0, jnp.sum(masked.reshape(groups, chunk, hidden_units), axis=1, keepdims=True))
    store_lines(gs_out, half, jnp.sum(
        (masked * normed).reshape(groups, chunk, hidden_units), axis=1, keepdims=True))


def tail_kernel(chunk, ndom, nrep, cores, z_ref, x_ref, st, gm, w2, dl, g2, out, acc):
    rows, hidden_units = z_ref.shape
    groups = rows // chunk
    half = st.shape[1] // 2
    z3 = z_ref[...].reshape(groups, chunk, hidden_units)
    rstd = load_lines(st, half, half)
    normed = (z3 - load_lines(st, 0, half)) * rstd
    back = by_lanes(dl[...], w2[...])
    masked = jnp.where(normed > 0, back.reshape(groups, chunk, hidden_units), 0.0)
    dpre = (masked - load_lines(gm, 0, half) - normed * load_lines(gm, half, half)) * rstd
    dpre = dpre.reshape(rows, hidden_units).astype(BF16)

    @pl.when(pl.program_id(0) == 0)
    def _():
        acc[...] = jnp.zeros_like(acc)

    acc[...] += lax.dot_general(x_ref[...], dpre, (((0,), (0,)), ((), ())), preferred_element_type=F32)

    @pl.when(pl.program_id(0) == pl.num_programs(0) - 1)
    def _():
        high, wide = acc.shape[0] // ndom, acc.shape[1] // nrep
        part, classes = g2.shape[0] // (ndom * nrep), g2.shape[1]
        for d in range(ndom):
            for r in range(nrep):
                first = acc[d * high:(d + 1) * high, r * wide:(r + 1) * wide]
                at = (r * ndom + d) * part
                second = jnp.concatenate(
                    [g2[at:at + part, :], jnp.zeros((part, wide - classes), F32)], axis=1)
                out[d % cores, d // cores, r] = jnp.concatenate([first, second], axis=0).astype(BF16)


def whole_spec(shape):
    return pl.BlockSpec(tuple(shape), lambda i: (0,) * len(shape))


def lead_spec(shape):
    return pl.BlockSpec(tuple(shape), lambda i: (i,) + (0,) * (len(shape) - 1))


def gather_rep(half, ndom, nrep, cores):
    dom, rep = lax.axis_index("dom"), lax.axis_index("rep")
    core = lax.rem(dom, cores)
    slots = jnp.zeros((nrep,) + half.shape, half.dtype)
    slots = lax.dynamic_update_slice(slots, half[None], (rep, 0, 0))
    for o in range(1, nrep):
        moved = lax.ppermute(half, "rep", [(s, (s + o) % nrep) for s in range(nrep)])
        slots = lax.dynamic_update_slice(slots, moved[None], (lax.rem(rep - o + nrep, nrep), 0, 0))
    theirs = lax.ppermute(slots, "dom", [(d, d + 1 - 2 * (d % 2)) for d in range(ndom)])
    both = jnp.zeros((cores,) + slots.shape, slots.dtype)
    both = lax.dynamic_update_slice(both, slots[None], (core, 0, 0, 0))
    return lax.dynamic_update_slice(both, theirs[None], (cores - 1 - core, 0, 0, 0))


def shards(hop_feats, adj_local, local_cols, adj_halo, halo_cols, boundary_rows, train_ids,
           shuffle, labels, labelled, w_first, w_second):
    ndom, nrep = lax.axis_size("dom"), lax.axis_size("rep")
    n = ndom * nrep
    cores = 2
    row_tiles, kl, tile, _ = adj_local.shape
    kh = adj_halo.shape[1]
    rows, width = hop_feats.shape[1:]
    slots = train_ids.shape[1]
    hidden_units, classes = w_second.shape[0] * nrep, w_second.shape[1]
    chunk = slots // n
    block = 256
    steps = slots // block
    groups = block // chunk
    wide = -(-n // 128) * 128
    big = pltpu.CompilerParams(vmem_limit_bytes=BIG)
    sds = jax.ShapeDtypeStruct

    core = lax.rem(lax.axis_index("dom"), cores)
    own_cols = hidden_units // nrep
    h1, h2 = w_first.shape[0] // cores, w_second.shape[0] // cores
    half = jnp.concatenate([
        lax.dynamic_slice(w_first, (core * h1, 0), (h1, own_cols)),
        jnp.pad(lax.dynamic_slice(w_second, (core * h2, 0), (h2, classes)),
                ((0, 0), (0, own_cols - classes)))], axis=0)
    both = gather_rep(half, ndom, nrep, cores)

    sent_block = boundary_rows.shape[1] // steps
    x3, tags, sent, own_counts = pl.pallas_call(
        functools.partial(pick_kernel, chunk),
        out_shape=(sds((slots, 3 * width), BF16), sds((slots, 128), F32),
                   sds((boundary_rows.shape[1], width), BF16), sds((1, wide), F32)),
        grid=(steps,),
        in_specs=[lead_spec((block, 1)), lead_spec((sent_block, 1)), whole_spec((1, slots)),
                  whole_spec((1, rows)), whole_spec((1, rows)), whole_spec(hop_feats.shape)],
        out_specs=(lead_spec((block, 3 * width)), lead_spec((block, 128)),
                   lead_spec((sent_block, width)), whole_spec((1, wide))),
        compiler_params=big, name="pick",
        cost_estimate=pl.CostEstimate(flops=2 * slots * rows * 5 * width, bytes_accessed=4 << 20, transcendentals=0),
    )(shuffle[0][:, None], boundary_rows[0][:, None], train_ids, labels[None], labelled[None], hop_feats)

    sent = sent.reshape(n, -1, width)
    halo, counts = comm_call(
        functools.partial(halo_kernel, ndom, nrep), (sds(sent.shape, BF16), sds((1, wide), F32)),
        [pltpu.VMEM(sent.shape, BF16), pltpu.VMEM((1, 1, wide), F32), pltpu.VMEM((n, 1, wide), F32)]
        + dma_sems(n, 4), "halo", 1, sent, own_counts)
    halo = halo.reshape(-1, tile, width)

    next_hop = pl.pallas_call(
        functools.partial(hop_kernel, kl, kh),
        out_shape=sds((row_tiles, tile, width), BF16),
        grid=(row_tiles,),
        in_specs=[
            pl.BlockSpec(memory_space=pltpu.SMEM), pl.BlockSpec(memory_space=pltpu.SMEM),
            lead_spec((1, kl, tile, tile)), lead_spec((1, kh, tile, tile)),
            pl.BlockSpec((1, row_tiles, tile, width), lambda i: (2, 0, 0, 0)), whole_spec(halo.shape)],
        out_specs=lead_spec((1, tile, width)),
        compiler_params=big, name="hop",
        cost_estimate=pl.CostEstimate(flops=2 * rows * width * tile * (kl + kh), bytes_accessed=9 << 20, transcendentals=0),
    )(local_cols, halo_cols, adj_local, adj_halo, hop_feats.reshape(3, row_tiles, tile, width), halo)
    next_hop = next_hop.reshape(rows, width)

    w1 = both[:, :, :h1].transpose(1, 0, 2, 3).reshape(nrep, cores * h1, own_cols)
    w2 = both[:, :, h1:, :classes].transpose(1, 0, 2, 3).reshape(hidden_units, classes)

    lines = 2 * hidden_units // 128
    x, z, stats = pl.pallas_call(
        functools.partial(pre_kernel, chunk),
        out_shape=(sds((slots, 4 * width), BF16), sds((slots, hidden_units), F32),
                   sds((n, lines, 128), F32)),
        grid=(steps,),
        in_specs=[lead_spec((block, 3 * width)), lead_spec((block, 128)), whole_spec((rows, width)),
                  whole_spec(w1.shape)],
        out_specs=(lead_spec((block, 4 * width)), lead_spec((block, hidden_units)),
                   lead_spec((groups, lines, 128))),
        compiler_params=big, name="pre",
    )(x3, tags, next_hop, w1)

    def combine(values, row, forward, cid):
        return comm_call(
            functools.partial(stats_kernel, ndom, nrep, forward, chunk),
            (sds((n, lines, 128), F32), sds((1, wide), F32)),
            [pltpu.VMEM((n, lines, 128), F32)] * 2
            + [pltpu.VMEM((1, 1, wide), F32), pltpu.VMEM((n, 1, wide), F32)] + dma_sems(n, 6),
            "stats_f" if forward else "stats_b", cid, values, row)

    stats, _ = combine(stats, own_counts, True, 2)

    line_spec = lead_spec((groups, lines, 128))
    dlogits, grad_two, gsums, losses = pl.pallas_call(
        functools.partial(head_kernel, chunk),
        out_shape=(sds((slots, classes), BF16), sds((hidden_units, classes), F32),
                   sds((n, lines, 128), F32), sds((1, wide), F32)),
        grid=(steps,),
        in_specs=[lead_spec((block, hidden_units)), lead_spec((block, 128)), line_spec,
                  whole_spec((1, wide)), whole_spec((1, wide)), whole_spec((hidden_units, classes))],
        out_specs=(lead_spec((block, classes)), whole_spec((hidden_units, classes)), line_spec,
                   whole_spec((1, wide))),
        compiler_params=big, name="head",
    )(z, tags, stats, counts, own_counts, w2)

    gmeans, turned = combine(gsums, losses, False, 3)
    loss = turned[:, :n]

    own_rows, part = 4 * width // ndom, hidden_units // n
    size = (nrep, own_rows + part, own_cols)
    packed = pl.pallas_call(
        functools.partial(tail_kernel, chunk, ndom, nrep, cores),
        out_shape=sds((cores, ndom // cores) + size, BF16),
        grid=(steps,),
        in_specs=[lead_spec((block, hidden_units)), lead_spec((block, 4 * width)), line_spec, line_spec,
                  whole_spec((hidden_units, classes)), lead_spec((block, classes)),
                  whole_spec((hidden_units, classes))],
        out_specs=whole_spec((cores, ndom // cores) + size),
        scratch_shapes=[pltpu.VMEM((4 * width, hidden_units), F32)],
        compiler_params=big, name="tail",
    )(z, x, stats, gmeans, w2, dlogits, grad_two)

    chips = ndom // cores
    first, second = comm_call(
        functools.partial(grads_kernel, ndom, nrep, cores, own_rows),
        (sds((own_rows, own_cols), F32), sds((ndom, part, own_cols), F32)),
        [pltpu.VMEM((chips,) + size, BF16), pltpu.VMEM((chips,) + size, BF16),
         pltpu.VMEM((chips - 1,) + size, BF16), pltpu.VMEM(size, BF16),
         pltpu.VMEM((nrep - 1,) + size[1:], BF16), pltpu.VMEM((ndom, part, own_cols), F32)]
        + dma_sems(chips, 4) + dma_sems(nrep, 2) + dma_sems(ndom, 2),
        "grads", 4, packed)
    second = second.reshape(ndom * part, own_cols)[:, :classes]
    return (next_hop, loss, first, second)


def solution(mesh):
    both = ("dom", "rep")
    placed = (
        P(None, both, None), P(both, None, None, None), P(both, None), P(both, None, None, None),
        P(both, None), P(both, None), P(both, None), P(both, None), P(both), P(both),
        P(None, "rep"), P("rep", None),
    )
    return jax.shard_map(
        shards, mesh=mesh, in_specs=placed,
        out_specs=(P(both, None), P(both, None), P("dom", "rep"), P("rep", None)),
        check_vma=False,
    )
```

time: 223 us -> 182 us (0.82)
  Pallas kernels: 180 us -> 154 us
  local copies, waits for them, and re-layouts: 19.2 us -> 11.8 us
  other arithmetic: 7.08 us -> 0.04 us
  waiting for transfers between devices: 2.26 us -> 6.49 us
  starting transfers between devices: 10.2 us -> 7.11 us
  matrix products: 2.61 us -> 0 us
    pallas_call x4, Pallas kernels: 124 us -> 88.7 us  [comm_call(): pl.pallas_call(kernel, out_shape=outs, in_specs=[pl.BlockSpec(memory_spac...]
    pallas_call x1 -> x2, Pallas kernels: 11.9 us -> 28.8 us  [the longest x1 16.5 us: shards(): pl.pallas_call(functools.partial(pick_kernel, chunk), out_shape=(sds((slo...]
    pallas_call x1, Pallas kernels: 18.7 us -> 10.8 us  [shards(): pl.pallas_call(functools.partial(pre_kernel, chunk), out_shape=(sds((slot...]
    reshape x7 -> x0, local copies, waits for them, and re-layouts: 7.81 us -> none  [the longest x2 4 us: combine(): values.reshape(n, lines, 128)]
    convert_element_type x3 -> x0, other arithmetic: 5.69 us -> none  [the longest x1 2.67 us: shards(): aux = aux.astype(F32).astype(BF16)]
    ppermute x6 -> x4, waiting for transfers between devices: 2.26 us -> 6.49 us  [the longest x3 6.49 us: gather_rep(): lax.ppermute(half, 'rep', [(s, (s + o) % nrep) for s in range(nrep)])]
    ppermute x6 -> x4, starting transfers between devices: 10.2 us -> 7.11 us  [the longest x3 7.04 us: gather_rep(): lax.ppermute(half, 'rep', [(s, (s + o) % nrep) for s in range(nrep)])]
    dot_general x1 -> x0, matrix products: 2.61 us -> none  [shards(): sent = jnp.dot(pick, hop_two, preferred_element_type=F32).astype(BF16)]
  transfers between devices with their start and end apart: 6 -> 4, of which waited for: 1 -> 1; matrix products, arithmetic and copies ran while one was open for 5% -> 3% of each run, Pallas kernels for 17% -> 25%
where the time goes in v2:
time: 182 us; the launch traced here: 181 us
  Pallas kernels  154 us (85%)
  local copies, waits for them, and re-layouts  11.8 us (6%)
  starting transfers between devices  7.11 us (4%)
  waiting for transfers between devices  6.49 us (4%)
    pallas_call x4, Pallas kernels, comm_call(): pl.pallas_call(kernel, out_shape=outs, in_specs=[pl.BlockSpec(memory_spac...  88.7 us
    pallas_call x1, Pallas kernels, shards(): pl.pallas_call(functools.partial(pick_kernel, chunk), out_shape=(sds((slo...  16.5 us
    pallas_call x1, Pallas kernels, shards(): pl.pallas_call(functools.partial(head_kernel, chunk), out_shape=(sds((slo...  13.6 us
    pallas_call x1, Pallas kernels, shards(): pl.pallas_call(functools.partial(hop_kernel, kl, kh), out_shape=sds((row_...  12.5 us
    pallas_call x1, Pallas kernels, shards(): pl.pallas_call(functools.partial(tail_kernel, chunk, ndom, nrep, cores),...  12.3 us
    pallas_call x1, Pallas kernels, shards(): pl.pallas_call(functools.partial(pre_kernel, chunk), out_shape=(sds((slot...  10.8 us
    ppermute x3, starting transfers between devices, gather_rep(): lax.ppermute(half, 'rep', [(s, (s + o) % nrep) for s in range(nrep)])  7.04 us
    ppermute x3, waiting for transfers between devices, gather_rep(): lax.ppermute(half, 'rep', [(s, (s + o) % nrep) for s in range(nrep)])  6.49 us
  transfers between devices with their start and end apart: 4, of which 1 were waited for; matrix products, arithmetic and copies ran while one was open for 3% of the time, Pallas kernels for 25%

profile of v2, /device:TPU:0, one launch (start us, length us, event | category | flops | bytes accessed | tf_op | source)
XLA Modules:
  0.0 180.6 jit_solution(11535708651187149357)
XLA Ops:
  0.6 0.0 copy-start
  0.7 0.8 constant_dynamic-slice_fusion
  1.5 0.1 copy.27
  1.6 0.0 copy-done
  1.7 3.1 %collective-permute-start = (bf16[384,256]{1,0:T(8,128)(2,1)S(1)}, bf16[384,256]{1,0:T(8,128)(2,1)S(1)}, u32[]{:S(2)}, u32[]{:S(2)}) collective-permute-start(bf16[384,256]{1,0:T(8,128)(2,1)S(1)} %fusion.1), channel_id=1, source_target_pairs={{0,1},{1,2},{2,3},{3,0},{4,5},{5,6},{6,7},{7,4},{8,9},{9,10},{10,1... | collective-permute-start | bytes 589832 | tf_op jit(solution)/shard_map/ppermute | solution.py:334
  4.8 2.6 %collective-permute-start.1 = (bf16[384,256]{1,0:T(8,128)(2,1)S(1)}, bf16[384,256]{1,0:T(8,128)(2,1)S(1)}, u32[]{:S(2)}, u32[]{:S(2)}) collective-permute-start(bf16[384,256]{1,0:T(8,128)(2,1)S(1)} %fusion.1), channel_id=1, source_target_pairs={{0,2},{1,3},{2,0},{3,1},{4,6},{5,7},{6,4},{7,5},{8,10},{9,11},{10,... | collective-permute-start | bytes 589832 | tf_op jit(solution)/shard_map/ppermute | solution.py:334
  7.4 1.3 collective-permute-start.2
  8.7 1.4 copy.22.hcols
  10.1 1.5 copy.21.bound
  11.6 2.0 %copy.20.shuf = s32[2048,1]{1,0:T(8,128)} copy(s32[2048,1]{0,1:T(1,128)} %bitcast.40) | data formatting | bytes 16384 | tf_op jit(solution)/shard_map/broadcast_in_dim;squeeze | solution.py:381
  13.6 0.1 broadcast_in_dim.33
  13.7 0.0 collective-permute-done
  13.8 6.5 %collective-permute-done.1 = bf16[384,256]{1,0:T(8,128)(2,1)S(1)} collective-permute-done((bf16[384,256]{1,0:T(8,128)(2,1)S(1)}, bf16[384,256]{1,0:T(8,128)(2,1)S(1)}, u32[]{:S(2)}, u32[]{:S(2)}) %collective-permute-start.1) | collective-permute-done | bytes 196640 | tf_op jit(solution)/shard_map/ppermute | solution.py:334
  20.3 0.0 collective-permute-done.2
  20.3 0.1 collective-permute-start.3
  20.4 16.5 %pick.1 = (bf16[2048,384]{1,0:T(8,128)(2,1)}, f32[2048,128]{1,0:T(8,128)}, bf16[512,128]{1,0:T(8,128)(2,1)}, f32[1,128]{1,0:T(1,128)}) custom-call(s32[2048,1]{1,0:T(8,128)} %copy.20.shuf, s32[512,1]{1,0:T(8,128)} %copy.21.bound, s32[1,2048]{1,0:T(1,128)} %ids.1, s32[1,2048]{1,0:T(1,128)} %bitcast.42, s32[1,2048]{1,0:T(1,128)} %bitcast.43, ...), custom_call_target="tpu_custom_call" | custom-call | flops 5368709120 | bytes 4194304 | tf_op jit(solution)/shard_map/pick/pallas_call | solution.py:370
  36.9 15.5 %halo.1 = (bf16[32,16,128]{2,1,0:T(8,128)(2,1)}, f32[1,128]{1,0:T(1,128)}) custom-call(bf16[32,16,128]{2,1,0:T(8,128)(2,1)} %bitcast.38, f32[1,128]{1,0:T(1,128)} %get-tuple-element.23.cnt.row.own_counts), custom_call_target="tpu_custom_call" | custom-call | tf_op jit(solution)/shard_map/halo/pallas_call | solution.py:53
  52.5 12.5 %hop.1 = bf16[16,128,128]{2,1,0:T(8,128)(2,1)} custom-call(s32[16,12]{1,0:T(8,128)} %lcols.1, s32[16,4]{1,0:T(8,128)} %copy.22.hcols, bf16[16,12,128,128]{3,2,1,0:T(8,128)(2,1)} %adj_l.1, bf16[16,4,128,128]{3,2,1,0:T(8,128)(2,1)} %adj_h.1, bf16[3,16,128,128]{3,2,1,0:T(8,128)(2,1)} %bitcast.36, bf16[4,128,128]{2,1,0:T(8,128)(2,1)} %bitcast.39), custom_call_target="tpu_custom_call" | custom-call | flops 1073741824 | bytes 9437184 | tf_op jit(solution)/shard_map/hop/pallas_call | solution.py:390
  64.9 0.1 broadcast_in_dim.32
  65.0 0.1 bitcast_dynamic-update-slice_fusion
  65.1 0.0 collective-permute-done.3
  65.1 0.1 bitcast_dynamic-update-slice_fusion.1
  65.2 0.9 slice.17
  66.0 1.0 slice.16
  67.1 10.8 %pre.1 = (bf16[2048,512]{1,0:T(8,128)(2,1)}, f32[2048,1024]{1,0:T(8,128)}, f32[32,16,128]{2,1,0:T(8,128)}) custom-call(bf16[2048,384]{1,0:T(8,128)(2,1)} %get-tuple-element.25.x3, f32[2048,128]{1,0:T(8,128)} %get-tuple-element.26.tag, bf16[2048,128]{1,0:T(8,128)(2,1)} %bitcast.34, bf16[4,512,256]{2,1,0:T(8,128)(2,1)} %bitcast.33), custom_call_target="tpu_custom_call" | custom-call | tf_op jit(solution)/shard_map/pre/pallas_call | solution.py:408
  77.8 23.0 %stats_f.1 = (f32[32,16,128]{2,1,0:T(8,128)}, f32[1,128]{1,0:T(1,128)}) custom-call(f32[32,16,128]{2,1,0:T(8,128)} %get-tuple-element.28.src, f32[1,128]{1,0:T(1,128)} %get-tuple-element.23.cnt.row.own_counts), custom_call_target="tpu_custom_call" | custom-call | tf_op jit(solution)/shard_map/stats_f/pallas_call | solution.py:53
  100.8 13.6 %head.1 = (bf16[2048,172]{1,0:T(8,128)(2,1)}, f32[1024,172]{1,0:T(8,128)}, f32[32,16,128]{2,1,0:T(8,128)}, f32[1,128]{1,0:T(1,128)}) custom-call(f32[2048,1024]{1,0:T(8,128)} %get-tuple-element.27.z_ref, f32[2048,128]{1,0:T(8,128)} %get-tuple-element.26.tag, f32[32,16,128]{2,1,0:T(8,128)} %get-tuple-element.29.st, f32[1,128]{1,0:T(1,128)} %get-tuple-element.30.counts, ...), custom_call_target="tpu_custom_call" | custom-call | tf_op jit(solution)/shard_map/head/pallas_call | solution.py:431
  114.4 22.2 %stats_b.1 = (f32[32,16,128]{2,1,0:T(8,128)}, f32[1,128]{1,0:T(1,128)}) custom-call(f32[32,16,128]{2,1,0:T(8,128)} %get-tuple-element.31.src, f32[1,128]{1,0:T(1,128)} %get-tuple-element.32.row), custom_call_target="tpu_custom_call" | custom-call | tf_op jit(solution)/shard_map/stats_b/pallas_call | solution.py:53
  136.6 12.3 %tail.1.src = bf16[2,4,4,96,256]{4,3,2,1,0:T(8,128)(2,1)} custom-call(f32[2048,1024]{1,0:T(8,128)} %get-tuple-element.27.z_ref, bf16[2048,512]{1,0:T(8,128)(2,1)} %get-tuple-element.34.x_ref, f32[32,16,128]{2,1,0:T(8,128)} %get-tuple-element.29.st, f32[32,16,128]{2,1,0:T(8,128)} %get-tuple-element.35.gm, bf16[1024,172]{1,0:T(8,128)(2,1)} %bitcast.32, ...), custom_call_target="tpu_custom_call" | custom-call | tf_op jit(solution)/shard_map/tail/pallas_call | solution.py:448
  148.9 0.0 copy-start.1
  148.9 28.0 %grads.1 = (f32[64,256]{1,0:T(8,128)}, f32[8,32,256]{2,1,0:T(8,128)}) custom-call(bf16[2,4,4,96,256]{4,3,2,1,0:T(8,128)(2,1)} %tail.1.src), custom_call_target="tpu_custom_call" | custom-call | tf_op jit(solution)/shard_map/grads/pallas_call | solution.py:53
  176.9 1.7 copy.26
  178.6 0.0 copy-done.1
  178.6 0.5 copy.36
  179.2 1.5 copy.37
  (6 shorter events, 0.1 us)
Async XLA Ops:
  0.6 1.0 copy-start
  1.7 12.1 %collective-permute-start = (bf16[384,256]{1,0:T(8,128)(2,1)S(1)}, bf16[384,256]{1,0:T(8,128)(2,1)S(1)}, u32[]{:S(2)}, u32[]{:S(2)}) collective-permute-start(bf16[384,256]{1,0:T(8,128)(2,1)S(1)} %fusion.1), channel_id=1, source_target_pairs={{0,1},{1,2},{2,3},{3,0},{4,5},{5,6},{6,7},{7,4},{8,9},{9,10},{10,1... | collective-permute-start | bytes 589832 | tf_op jit(solution)/shard_map/ppermute | solution.py:334
  4.8 15.5 %collective-permute-start.1 = (bf16[384,256]{1,0:T(8,128)(2,1)S(1)}, bf16[384,256]{1,0:T(8,128)(2,1)S(1)}, u32[]{:S(2)}, u32[]{:S(2)}) collective-permute-start(bf16[384,256]{1,0:T(8,128)(2,1)S(1)} %fusion.1), channel_id=1, source_target_pairs={{0,2},{1,3},{2,0},{3,1},{4,6},{5,7},{6,4},{7,5},{8,10},{9,11},{10,... | collective-permute-start | bytes 589832 | tf_op jit(solution)/shard_map/ppermute | solution.py:334
  7.4 12.9 %collective-permute-start.2 = (bf16[384,256]{1,0:T(8,128)(2,1)S(1)}, bf16[384,256]{1,0:T(8,128)(2,1)S(1)}, u32[]{:S(2)}, u32[]{:S(2)}) collective-permute-start(bf16[384,256]{1,0:T(8,128)(2,1)S(1)} %fusion.1), channel_id=1, source_target_pairs={{0,3},{1,0},{2,1},{3,2},{4,7},{5,4},{6,5},{7,6},{8,11},{9,8},{10,9... | collective-permute-start | bytes 589832 | tf_op jit(solution)/shard_map/ppermute | solution.py:334
  20.3 44.8 %collective-permute-start.3 = (bf16[4,384,256]{2,1,0:T(8,128)(2,1)S(1)}, bf16[4,384,256]{2,1,0:T(8,128)(2,1)S(1)}, u32[]{:S(2)}, u32[]{:S(2)}) collective-permute-start(bf16[4,384,256]{2,1,0:T(8,128)(2,1)S(1)} %bitcast_dynamic-update-slice_fusion.2), channel_id=1, source_target_pairs={{0,4},{4,0},{8,12},{12,8},{16,20},{20,16},{24,28},{28,24},{1,5},{5... | collective-permute-start | bytes 2359304 | tf_op jit(solution)/shard_map/ppermute | solution.py:336
  148.9 29.7 %copy-start.1 = (f32[1,128]{1,0:T(1,128)S(1)}, f32[1,128]{1,0:T(1,128)}, u32[]{:S(2)}) copy-start(f32[1,128]{1,0:T(1,128)} %get-tuple-element.33) | copy-start | bytes 1540

commit v3 on v2

--- a/solution.py
+++ b/solution.py
@@ -125,7 +125,7 @@
     out[...] = gath[...]
 
 
-def grads_kernel(ndom, nrep, cores, split, src, out1, out2, recv0, sum0, recv1, sum1, recv2, gath,
+def grads_kernel(ndom, nrep, cores, split, src, out1, out2, recv0, sum0, recv1, sum1, kept, recv2, gath,
                  s0, r0, s1, r1, s2, r2, s3, r3):
     dom, rep = lax.axis_index("dom"), lax.axis_index("rep")
     me = dom * nrep + rep
@@ -154,17 +154,18 @@
         return to(sum0.at[peer], recv1.at[o - 1], s1.at[o], r1.at[o], peer * cores + core, rep)
 
     run([near(o) for o in range(1, chips)])
-    total = sum0[chip].astype(F32)
+    total = src[core, chip].astype(F32) + recv0[chip].astype(F32)
     for o in range(1, chips):
         total = total + recv1[o - 1].astype(F32)
     sum1[...] = total.astype(BF16)
+    kept[...] = total
 
     def along(o):
         peer = lax.rem(rep + o, nrep)
         return to(sum1.at[peer], recv2.at[o - 1], s2.at[o], r2.at[o], dom, peer)
 
     run([along(o) for o in range(1, nrep)])
-    total = sum1[rep].astype(F32)
+    total = kept[rep]
     for o in range(1, nrep):
         total = total + recv2[o - 1].astype(F32)
     out1[...] = total[:split]
@@ -325,14 +326,17 @@
     return pl.BlockSpec(tuple(shape), lambda i: (i,) + (0,) * (len(shape) - 1))
 
 
-def gather_rep(half, ndom, nrep, cores):
+def send_rep(half, nrep):
+    return [lax.ppermute(half, "rep", [(s, (s + o) % nrep) for s in range(nrep)]) for o in range(1, nrep)]
+
+
+def gather_rep(half, arrived, ndom, nrep, cores):
     dom, rep = lax.axis_index("dom"), lax.axis_index("rep")
     core = lax.rem(dom, cores)
     slots = jnp.zeros((nrep,) + half.shape, half.dtype)
     slots = lax.dynamic_update_slice(slots, half[None], (rep, 0, 0))
     for o in range(1, nrep):
-        moved = lax.ppermute(half, "rep", [(s, (s + o) % nrep) for s in range(nrep)])
-        slots = lax.dynamic_update_slice(slots, moved[None], (lax.rem(rep - o + nrep, nrep), 0, 0))
+        slots = lax.dynamic_update_slice(slots, arrived[o - 1][None], (lax.rem(rep - o + nrep, nrep), 0, 0))
     theirs = lax.ppermute(slots, "dom", [(d, d + 1 - 2 * (d % 2)) for d in range(ndom)])
     both = jnp.zeros((cores,) + slots.shape, slots.dtype)
     both = lax.dynamic_update_slice(both, slots[None], (core, 0, 0, 0))
@@ -364,7 +368,7 @@
         lax.dynamic_slice(w_first, (core * h1, 0), (h1, own_cols)),
         jnp.pad(lax.dynamic_slice(w_second, (core * h2, 0), (h2, classes)),
                 ((0, 0), (0, own_cols - classes)))], axis=0)
-    both = gather_rep(half, ndom, nrep, cores)
+    arrived = send_rep(half, nrep)
 
     sent_block = boundary_rows.shape[1] // steps
     x3, tags, sent, own_counts = pl.pallas_call(
@@ -380,6 +384,8 @@
         cost_estimate=pl.CostEstimate(flops=2 * slots * rows * 5 * width, bytes_accessed=4 << 20, transcendentals=0),
     )(shuffle[0][:, None], boundary_rows[0][:, None], train_ids, labels[None], labelled[None], hop_feats)
 
+    arrived, own_counts = lax.optimization_barrier((arrived, own_counts))
+    both = gather_rep(half, arrived, ndom, nrep, cores)
     sent = sent.reshape(n, -1, width)
     halo, counts = comm_call(
         functools.partial(halo_kernel, ndom, nrep), (sds(sent.shape, BF16), sds((1, wide), F32)),
@@ -462,7 +468,7 @@
         functools.partial(grads_kernel, ndom, nrep, cores, own_rows),
         (sds((own_rows, own_cols), F32), sds((ndom, part, own_cols), F32)),
         [pltpu.VMEM((chips,) + size, BF16), pltpu.VMEM((chips,) + size, BF16),
-         pltpu.VMEM((chips - 1,) + size, BF16), pltpu.VMEM(size, BF16),
+         pltpu.VMEM((chips - 1,) + size, BF16), pltpu.VMEM(size, BF16), pltpu.VMEM(size, F32),
          pltpu.VMEM((nrep - 1,) + size[1:], BF16), pltpu.VMEM((ndom, part, own_cols), F32)]
         + dma_sems(chips, 4) + dma_sems(nrep, 2) + dma_sems(ndom, 2),
         "grads", 4, packed)

time: 182 us -> 172 us (0.945)
  waiting for transfers between devices: 6.49 us -> 0.01 us
  Pallas kernels: 154 us -> 152 us
    ppermute x3, waiting for transfers between devices: 6.49 us -> 0.01 us  [send_rep(): lax.ppermute(half, 'rep', [(s, (s + o) % nrep) for s in range(nrep)])]
    pallas_call x4, Pallas kernels: 88.7 us -> 86.3 us  [comm_call(): pl.pallas_call(kernel, out_shape=outs, in_specs=[pl.BlockSpec(memory_spac...]
    unnamed x9 -> x11, local copies, waits for them, and re-layouts: 5.19 us -> 4.88 us
  transfers between devices with their start and end apart: 4 -> 4, of which waited for: 1 -> 0; matrix products, arithmetic and copies ran while one was open for 3% -> 3% of each run, Pallas kernels for 25% -> 25%
where the time goes in v3:
time: 172 us; the launch traced here: 171 us
  Pallas kernels  152 us (88%)
  local copies, waits for them, and re-layouts  11.5 us (7%)
  starting transfers between devices  6.21 us (4%)
    pallas_call x4, Pallas kernels, comm_call(): pl.pallas_call(kernel, out_shape=outs, in_specs=[pl.BlockSpec(memory_spac...  86.3 us
    pallas_call x1, Pallas kernels, shards(): pl.pallas_call(functools.partial(pick_kernel, chunk), out_shape=(sds((slo...  16.5 us
    pallas_call x1, Pallas kernels, shards(): pl.pallas_call(functools.partial(head_kernel, chunk), out_shape=(sds((slo...  13.6 us
    pallas_call x1, Pallas kernels, shards(): pl.pallas_call(functools.partial(hop_kernel, kl, kh), out_shape=sds((row_...  12.5 us
    pallas_call x1, Pallas kernels, shards(): pl.pallas_call(functools.partial(tail_kernel, chunk, ndom, nrep, cores),...  12.3 us
    pallas_call x1, Pallas kernels, shards(): pl.pallas_call(functools.partial(pre_kernel, chunk), out_shape=(sds((slot...  10.8 us
    ppermute x3, starting transfers between devices, send_rep(): lax.ppermute(half, 'rep', [(s, (s + o) % nrep) for s in range(nrep)])  6.14 us
    unnamed x11, local copies, waits for them, and re-layouts  4.88 us
  transfers between devices with their start and end apart: 4, of which 0 were waited for; matrix products, arithmetic and copies ran while one was open for 3% of the time, Pallas kernels for 25%

profile of v3, /device:TPU:0, one launch (start us, length us, event | category | flops | bytes accessed | tf_op | source)
XLA Modules:
  0.0 170.5 jit_solution(17496240912202651530)
XLA Ops:
  0.6 0.0 copy-start
  0.7 0.8 constant_dynamic-slice_fusion
  1.5 0.1 copy.27
  1.6 0.0 copy-done
  1.7 5.1 %collective-permute-start.2 = (bf16[384,256]{1,0:T(8,128)(2,1)S(1)}, bf16[384,256]{1,0:T(8,128)(2,1)S(1)}, u32[]{:S(2)}, u32[]{:S(2)}) collective-permute-start(bf16[384,256]{1,0:T(8,128)(2,1)S(1)} %fusion.1), channel_id=1, source_target_pairs={{0,3},{1,0},{2,1},{3,2},{4,7},{5,4},{6,5},{7,6},{8,11},{9,8},{10,9... | collective-permute-start | bytes 589832 | tf_op jit(solution)/shard_map/ppermute | solution.py:330
  6.8 0.0 collective-permute-start.1
  6.8 1.0 collective-permute-start
  7.8 1.5 copy.21.bound
  9.4 2.0 %copy.20.shuf = s32[2048,1]{1,0:T(8,128)} copy(s32[2048,1]{0,1:T(1,128)} %bitcast.40) | data formatting | bytes 16384 | tf_op jit(solution)/shard_map/broadcast_in_dim;squeeze | solution.py:385
  11.4 16.5 %pick.1 = (bf16[2048,384]{1,0:T(8,128)(2,1)}, f32[2048,128]{1,0:T(8,128)}, bf16[512,128]{1,0:T(8,128)(2,1)}, f32[1,128]{1,0:T(1,128)}) custom-call(s32[2048,1]{1,0:T(8,128)} %copy.20.shuf, s32[512,1]{1,0:T(8,128)} %copy.21.bound, s32[1,2048]{1,0:T(1,128)} %ids.1, s32[1,2048]{1,0:T(1,128)} %bitcast.42, s32[1,2048]{1,0:T(1,128)} %bitcast.43, ...), custom_call_target="tpu_custom_call" | custom-call | flops 5368709120 | bytes 4194304 | tf_op jit(solution)/shard_map/pick/pallas_call | solution.py:374
  27.9 0.0 copy-start.1
  27.9 0.1 broadcast_in_dim.33
  28.0 0.0 collective-permute-done.2
  28.0 0.0 collective-permute-done.1
  28.0 0.0 collective-permute-done
  28.1 0.1 collective-permute-start.3
  28.2 0.4 copy-done.1
  28.6 0.7 copy.23.hcols
  29.3 13.1 %halo.1 = (bf16[32,16,128]{2,1,0:T(8,128)(2,1)}, f32[1,128]{1,0:T(1,128)}) custom-call(bf16[32,16,128]{2,1,0:T(8,128)(2,1)} %bitcast.38, f32[1,128]{1,0:T(1,128)} %get-tuple-element.28.cnt.row.own_counts), custom_call_target="tpu_custom_call" | custom-call | tf_op jit(solution)/shard_map/halo/pallas_call | solution.py:53
  42.4 12.5 %hop.1 = bf16[16,128,128]{2,1,0:T(8,128)(2,1)} custom-call(s32[16,12]{1,0:T(8,128)} %lcols.1, s32[16,4]{1,0:T(8,128)} %copy.23.hcols, bf16[16,12,128,128]{3,2,1,0:T(8,128)(2,1)} %adj_l.1, bf16[16,4,128,128]{3,2,1,0:T(8,128)(2,1)} %adj_h.1, bf16[3,16,128,128]{3,2,1,0:T(8,128)(2,1)} %bitcast.36, bf16[4,128,128]{2,1,0:T(8,128)(2,1)} %bitcast.39), custom_call_target="tpu_custom_call" | custom-call | flops 1073741824 | bytes 9437184 | tf_op jit(solution)/shard_map/hop/pallas_call | solution.py:396
  54.9 0.1 broadcast_in_dim.32
  55.0 0.1 bitcast_dynamic-update-slice_fusion
  55.0 0.0 collective-permute-done.3
  55.0 0.1 bitcast_dynamic-update-slice_fusion.1
  55.1 0.9 slice.17
  56.0 1.1 slice.16
  57.0 10.8 %pre.1 = (bf16[2048,512]{1,0:T(8,128)(2,1)}, f32[2048,1024]{1,0:T(8,128)}, f32[32,16,128]{2,1,0:T(8,128)}) custom-call(bf16[2048,384]{1,0:T(8,128)(2,1)} %get-tuple-element.30.x3, f32[2048,128]{1,0:T(8,128)} %get-tuple-element.31.tag, bf16[2048,128]{1,0:T(8,128)(2,1)} %bitcast.34, bf16[4,512,256]{2,1,0:T(8,128)(2,1)} %bitcast.33), custom_call_target="tpu_custom_call" | custom-call | tf_op jit(solution)/shard_map/pre/pallas_call | solution.py:414
  67.8 22.4 %stats_f.1 = (f32[32,16,128]{2,1,0:T(8,128)}, f32[1,128]{1,0:T(1,128)}) custom-call(f32[32,16,128]{2,1,0:T(8,128)} %get-tuple-element.36.src, f32[1,128]{1,0:T(1,128)} %get-tuple-element.28.cnt.row.own_counts), custom_call_target="tpu_custom_call" | custom-call | tf_op jit(solution)/shard_map/stats_f/pallas_call | solution.py:53
  90.2 13.6 %head.1 = (bf16[2048,172]{1,0:T(8,128)(2,1)}, f32[1024,172]{1,0:T(8,128)}, f32[32,16,128]{2,1,0:T(8,128)}, f32[1,128]{1,0:T(1,128)}) custom-call(f32[2048,1024]{1,0:T(8,128)} %get-tuple-element.35.z_ref, f32[2048,128]{1,0:T(8,128)} %get-tuple-element.31.tag, f32[32,16,128]{2,1,0:T(8,128)} %get-tuple-element.37.st, f32[1,128]{1,0:T(1,128)} %get-tuple-element.38.counts, ...), custom_call_target="tpu_custom_call" | custom-call | tf_op jit(solution)/shard_map/head/pallas_call | solution.py:437
  103.7 22.9 %stats_b.1 = (f32[32,16,128]{2,1,0:T(8,128)}, f32[1,128]{1,0:T(1,128)}) custom-call(f32[32,16,128]{2,1,0:T(8,128)} %get-tuple-element.39.src, f32[1,128]{1,0:T(1,128)} %get-tuple-element.40.row), custom_call_target="tpu_custom_call" | custom-call | tf_op jit(solution)/shard_map/stats_b/pallas_call | solution.py:53
  126.7 12.3 %tail.1.src = bf16[2,4,4,96,256]{4,3,2,1,0:T(8,128)(2,1)} custom-call(f32[2048,1024]{1,0:T(8,128)} %get-tuple-element.35.z_ref, bf16[2048,512]{1,0:T(8,128)(2,1)} %get-tuple-element.42.x_ref, f32[32,16,128]{2,1,0:T(8,128)} %get-tuple-element.37.st, f32[32,16,128]{2,1,0:T(8,128)} %get-tuple-element.43.gm, bf16[1024,172]{1,0:T(8,128)(2,1)} %bitcast.32, ...), custom_call_target="tpu_custom_call" | custom-call | tf_op jit(solution)/shard_map/tail/pallas_call | solution.py:454
  138.9 0.0 copy-start.2
  138.9 27.9 %grads.1 = (f32[64,256]{1,0:T(8,128)}, f32[8,32,256]{2,1,0:T(8,128)}) custom-call(bf16[2,4,4,96,256]{4,3,2,1,0:T(8,128)(2,1)} %tail.1.src), custom_call_target="tpu_custom_call" | custom-call | tf_op jit(solution)/shard_map/grads/pallas_call | solution.py:53
  166.8 1.7 %copy.26 = f32[256,172]{0,1:T(8,128)} copy(f32[256,172]{1,0:T(8,128)} %bitcast.37) | data formatting | bytes 352256
  168.5 0.0 copy-done.2
  168.6 0.5 copy.36
  169.1 1.5 copy.37
  (6 shorter events, 0.1 us)
Async XLA Ops:
  0.6 1.0 copy-start
  1.7 26.4 %collective-permute-start.2 = (bf16[384,256]{1,0:T(8,128)(2,1)S(1)}, bf16[384,256]{1,0:T(8,128)(2,1)S(1)}, u32[]{:S(2)}, u32[]{:S(2)}) collective-permute-start(bf16[384,256]{1,0:T(8,128)(2,1)S(1)} %fusion.1), channel_id=1, source_target_pairs={{0,3},{1,0},{2,1},{3,2},{4,7},{5,4},{6,5},{7,6},{8,11},{9,8},{10,9... | collective-permute-start | bytes 589832 | tf_op jit(solution)/shard_map/ppermute | solution.py:330
  6.8 21.2 %collective-permute-start.1 = (bf16[384,256]{1,0:T(8,128)(2,1)S(1)}, bf16[384,256]{1,0:T(8,128)(2,1)S(1)}, u32[]{:S(2)}, u32[]{:S(2)}) collective-permute-start(bf16[384,256]{1,0:T(8,128)(2,1)S(1)} %fusion.1), channel_id=1, source_target_pairs={{0,2},{1,3},{2,0},{3,1},{4,6},{5,7},{6,4},{7,5},{8,10},{9,11},{10,... | collective-permute-start | bytes 589832 | tf_op jit(solution)/shard_map/ppermute | solution.py:330
  6.8 21.2 %collective-permute-start = (bf16[384,256]{1,0:T(8,128)(2,1)S(1)}, bf16[384,256]{1,0:T(8,128)(2,1)S(1)}, u32[]{:S(2)}, u32[]{:S(2)}) collective-permute-start(bf16[384,256]{1,0:T(8,128)(2,1)S(1)} %fusion.1), channel_id=1, source_target_pairs={{0,1},{1,2},{2,3},{3,0},{4,5},{5,6},{6,7},{7,4},{8,9},{9,10},{10,1... | collective-permute-start | bytes 589832 | tf_op jit(solution)/shard_map/ppermute | solution.py:330
  27.9 0.7 copy-start.1
  28.1 26.9 %collective-permute-start.3 = (bf16[4,384,256]{2,1,0:T(8,128)(2,1)S(1)}, bf16[4,384,256]{2,1,0:T(8,128)(2,1)S(1)}, u32[]{:S(2)}, u32[]{:S(2)}) collective-permute-start(bf16[4,384,256]{2,1,0:T(8,128)(2,1)S(1)} %bitcast_dynamic-update-slice_fusion.2), channel_id=1, source_target_pairs={{0,4},{4,0},{8,12},{12,8},{16,20},{20,16},{24,28},{28,24},{1,5},{5... | collective-permute-start | bytes 2359304 | tf_op jit(solution)/shard_map/ppermute | solution.py:340
  138.9 29.6 %copy-start.2 = (f32[1,128]{1,0:T(1,128)S(1)}, f32[1,128]{1,0:T(1,128)}, u32[]{:S(2)}) copy-start(f32[1,128]{1,0:T(1,128)} %get-tuple-element.41) | copy-start | bytes 1540
